TPU v7x, 256 devices: a whole 4x4x8 slice. The times are simulated.
256 devices in a mesh: dp: 16 (over x_lo, z), fsdp: 16 (over y, x_hi, core).
Axes of the slice: x: 4 (x_hi: 2, x_lo: 2; x = x_hi * 2 + x_lo), y: 4, z: 8, core: 2. Of those that a mesh axis runs over, the one named last changes fastest.
Arguments:
- hidden_states: bfloat16 [32768, 8192], P(('dp', 'fsdp')), may hold values from -450 to 450
- gain: float32 [8192], replicated, may hold values from 0.1 to 1.9
- key_weight: bfloat16 [8192, 512], P('fsdp'), may hold values from -0.0625 to 0.0625
- key_cotangent: bfloat16 [32768, 512], P(('dp', 'fsdp')), may hold values from -18 to 18
- bucket: int32 [5, 32768], P(None, 'fsdp'), may hold values from 0 to 255
- sign_bits: int32 [5, 32768], P(None, 'fsdp'), may hold values from 0 to 1
- momentum: float32 [16, 5, 32768], P('fsdp', None, 'dp'), may hold values from -12 to 12
- error: float32 [16, 5, 32768], P('fsdp', None, 'dp'), may hold values from -12 to 12
Outputs:
- hidden_grad: bfloat16 [32768, 8192], P(('dp', 'fsdp'))
- momentum_new: float32 [16, 5, 32768], P('fsdp', None, 'dp')
- error_new: float32 [16, 5, 32768], P('fsdp', None, 'dp')
- update: float32 [8192, 512], P('fsdp')
All inputs are finite; a program needn't handle non-finite values.
Results may differ from a plain program's by a relative error of at most 0.0095.
Values may be sent and summed in bfloat16 or wider, within the bound.
A program may use at most 128 MiB of HBM per device.

v0:
```python
import math

import jax
import jax.numpy as jnp
from jax import lax
from jax.sharding import PartitionSpec as P

ROWS = 5
NBB = 256
BLOCK = 128


EPS = 1e-05
DECAY = 0.9
THRESHOLD = 1.0


def normalize(states, gain):
    values = states.astype(jnp.float32)
    inverse_rms = lax.rsqrt(jnp.mean(values * values, axis=1, keepdims=True) + EPS)
    normed = values * inverse_rms
    return (normed, inverse_rms, (normed * gain).astype(jnp.bfloat16))


def norm_backward(input_grad, gain, normed, inverse_rms):
    scaled = input_grad.astype(jnp.float32) * gain
    mean_term = jnp.mean(scaled * normed, axis=1, keepdims=True)
    return (inverse_rms * (scaled - normed * mean_term)).astype(jnp.bfloat16)


def split_product(selector, values, numbers):
    upper = values.astype(jnp.bfloat16)
    lower = (values - upper.astype(jnp.float32)).astype(jnp.bfloat16)
    first = lax.dot_general(selector, upper, numbers, preferred_element_type=jnp.float32)
    return first + lax.dot_general(selector, lower, numbers, preferred_element_type=jnp.float32)


def middle_three(first, second, third):
    return jnp.maximum(jnp.minimum(first, second), jnp.minimum(jnp.maximum(first, second), third))


def middle_five(items):
    upper_pair = jnp.minimum(jnp.maximum(items[0], items[1]), jnp.maximum(items[2], items[3]))
    lower_pair = jnp.maximum(jnp.minimum(items[0], items[1]), jnp.minimum(items[2], items[3]))
    return middle_three(items[4], upper_pair, lower_pair)


def on_device(hidden_states, gain, key_weight, key_cotangent, bucket, sign_bits, momentum, error):
    normed, inverse_rms, inputs = normalize(hidden_states, gain)
    fsdp_count = lax.axis_size("fsdp")
    dp_count = lax.axis_size("dp")
    local_rows = key_weight.shape[0]
    grad_scale = 1.0 / math.sqrt(inputs.shape[0] * fsdp_count)
    contract_last = (((1,), (1,)), ((), ()))
    contract_first = (((0,), (0,)), ((), ()))
    contract_plain = (((1,), (0,)), ((), ()))
    input_grad = lax.dot_general(
        key_cotangent,
        lax.all_gather(key_weight, "fsdp", axis=0, tiled=True),
        contract_last,
        preferred_element_type=jnp.float32,
    ).astype(jnp.bfloat16)
    weight_grad = lax.psum_scatter(
        lax.dot_general(inputs, key_cotangent, contract_first, preferred_element_type=jnp.float32),
        "fsdp",
        scatter_dimension=0,
        tiled=True,
    )
    hidden_grad = norm_backward(input_grad, gain, normed, inverse_rms)
    blocks = (weight_grad * grad_scale).reshape(-1, BLOCK)
    signs = (2 * sign_bits - 1).astype(jnp.bfloat16)
    sign_values = (2 * sign_bits - 1).astype(jnp.float32)
    zero_sel = jnp.zeros((), jnp.bfloat16)
    bucket_ids = lax.broadcasted_iota(jnp.int32, (NBB, 1), 0)
    local_table = jnp.stack(
        [
            split_product(
                jnp.where(
                    bucket[row_index][None, :] == bucket_ids, signs[row_index][None, :], zero_sel
                ),
                blocks,
                contract_plain,
            )
            for row_index in range(ROWS)
        ]
    ).reshape(1, ROWS, NBB * BLOCK)
    share = momentum.shape[2]
    offset = lax.axis_index("dp") * share
    total = lax.psum(local_table, "dp")
    momentum_all, error_all = (
        lax.all_gather(momentum, "dp", axis=2, tiled=True),
        lax.all_gather(error, "dp", axis=2, tiled=True),
    )
    momentum_all = DECAY * momentum_all + total / dp_count
    error_all = error_all + momentum_all
    momentum_new = lax.dynamic_slice_in_dim(momentum_all, offset, share, 2)
    error_mid = lax.dynamic_slice_in_dim(error_all, offset, share, 2)
    error_rows = error_all.reshape(ROWS, NBB, BLOCK)
    reads = [
        error_rows[row_index][bucket[row_index]] * sign_values[row_index][:, None]
        for row_index in range(ROWS)
    ]
    estimate = middle_five(reads)
    update = estimate - jnp.clip(estimate, -THRESHOLD, THRESHOLD)
    share_buckets = share // BLOCK
    share_ids = bucket_ids[:share_buckets] + lax.axis_index("dp") * share_buckets
    sketched = jnp.stack(
        [
            split_product(
                jnp.where(
                    bucket[row_index][None, :] == share_ids, signs[row_index][None, :], zero_sel
                ),
                update,
                contract_plain,
            )
            for row_index in range(ROWS)
        ]
    ).reshape(1, ROWS, share)
    error_new = error_mid - sketched
    return (hidden_grad, momentum_new, error_new, update.reshape(local_rows, -1))


def solution(mesh):
    in_specs = (
        P(("dp", "fsdp"), None),
        P(),
        P("fsdp", None),
        P(("dp", "fsdp"), None),
        P(None, "fsdp"),
        P(None, "fsdp"),
        P("fsdp", None, "dp"),
        P("fsdp", None, "dp"),
    )
    out_specs = (
        P(("dp", "fsdp"), None),
        P("fsdp", None, "dp"),
        P("fsdp", None, "dp"),
        P("fsdp", None),
    )
    return jax.shard_map(
        on_device, mesh=mesh, in_specs=in_specs, out_specs=out_specs, check_vma=False
    )
```

profile of v0, /device:TPU:8, one launch (start us, length us, event | category | flops | bytes accessed | tf_op | source)
XLA Modules:
  0.0 459.5 jit_solution(4730571802656826122)
XLA Ops:
  7.2 0.7 all-gather.2.cloned.1.call-update
  8.0 2.1 fusion.10
  10.1 8.2 %fusion.11 = f32[8192,512]{1,0:T(8,128)} fusion(bf16[128,512]{1,0:T(8,128)(2,1)S(1)} %copy-done, bf16[128,8192]{1,0:T(8,128)(2,1)S(1)} %copy-done.1, f32[8192]{0:T(1024)S(1)} %copy-done.18, f32[128]{0:T(128)S(1)} %add_rsqrt_fusion), kind=kOutput, calls=%fused_computation.19 | convolution fusion | flops 1077936128 | bytes 19038720 | tf_op jit(solution)/shard_map/dot_general | solution.py:64
  18.4 0.7 copy-done.26
  19.2 0.7 slice_reduce_fusion.7
  19.8 1.0 mul.191
  20.8 1.0 mul.195
  21.8 1.0 mul.199
  22.7 1.0 mul.203
  23.7 1.0 mul.207
  24.7 0.5 fusion.132
  25.5 0.6 broadcast_clamp_fusion.4
  26.1 0.6 broadcast_clamp_fusion.3
  26.7 0.6 broadcast_clamp_fusion.2
  27.3 0.6 broadcast_clamp_fusion.1
  27.9 0.6 broadcast_clamp_fusion
  28.5 42.3 %all_gather.10 = f32[1,5,32768]{2,0,1:T(1,128)} all-gather(f32[1,5,2048]{2,0,1:T(1,128)S(1)} %copy-done.28), channel_id=1, replica_groups=mesh['dp'=16,'fsdp'=16] {'dp'}, dimensions={2}, use_global_device_ids=true | all-gather | bytes 696320 | tf_op jit(solution)/shard_map/all_gather | solution.py:91
  70.8 36.0 %all_gather.11 = f32[1,5,32768]{2,0,1:T(1,128)} all-gather(f32[1,5,2048]{2,0,1:T(1,128)S(1)} %copy-done.29), channel_id=1, replica_groups=mesh['dp'=16,'fsdp'=16] {'dp'}, dimensions={2}, use_global_device_ids=true | all-gather | bytes 696320 | tf_op jit(solution)/shard_map/all_gather | solution.py:92
  106.9 9.1 %fusion.5 = (f32[128]{0:T(128)S(1)}, f32[128,8192]{1,0:T(8,128)}) fusion(bf16[128,8192]{1,0:T(8,128)(2,1)S(1)} %copy-done.1, f32[128]{0:T(128)S(1)} %add_rsqrt_fusion, f32[8192]{0:T(1024)S(1)} %copy-done.18, bf16[128,512]{1,0:T(8,128)(2,1)S(1)} %copy-done, bf16[8192,512]{1,0:T(8,128)(2,1)} %all-gather.2.cloned.1.call-done), kind=kOutput, calls=%fused_computation.13 | convolution fusion | flops 1081081728 | bytes 14844928 | tf_op jit(solution)/shard_map/dot_general | solution.py:57
  116.0 0.5 broadcast_multiply_fusion.1
  116.5 133.0 %reduce-scatter.2.cloned.1.call-done = f32[512,512]{1,0:T(8,128)} async-done(((f32[8192,512]{1,0:T(8,128)}), f32[512,512]{1,0:T(8,128)}) %reduce-scatter.2.cloned.1.call-update) | async-done | bytes 1048592 | tf_op jit(solution)/shard_map/reduce_scatter | solution.py:63
  249.6 2.3 broadcast_multiply_fusion
  251.9 1.3 reshape.223
  253.3 0.4 fusion.32
  253.8 0.4 fusion.43
  254.2 0.4 fusion.36
  254.6 0.4 fusion.40
  255.1 0.4 fusion.28
  255.5 0.4 fusion.46
  255.9 0.4 fusion.24
  256.4 0.4 fusion.49
  256.8 0.4 fusion.20
  257.3 0.4 fusion.52
  257.8 0.8 copy-done.17
  258.7 4.5 fusion.8
  263.2 131.6 %all-reduce.2.cloned.1.call-done = f32[1,5,32768]{2,0,1:T(1,128)} async-done(((f32[1,5,32768]{2,0,1:T(1,128)}), f32[1,5,32768]{2,0,1:T(1,128)}) %all-reduce.2.cloned.1.call-update) | async-done | bytes 655376 | tf_op jit(solution)/shard_map/psum | solution.py:89
  394.7 3.5 fusion.153
  398.3 5.7 %gather_fusion = f32[2048,128]{1,0:T(8,128)S(1)} fusion(f32[256,128]{1,0:T(8,128)S(1)} %bitcast.114, s32[2048]{0:T(1024)S(1)} %copy-done.48), kind=kCustom, calls=%fused_computation | custom fusion | bytes 2105344 | tf_op jit(solution)/shard_map/gather | solution.py:100
  404.0 1.2 gather.30
  405.2 5.5 %gather_fusion.1 = f32[2048,128]{1,0:T(8,128)S(1)} fusion(f32[256,128]{1,0:T(8,128)S(1)} %bitcast.113, s32[2048]{0:T(1024)S(1)} %copy-done.47), kind=kCustom, calls=%fused_computation.1 | custom fusion | bytes 2105344 | tf_op jit(solution)/shard_map/gather | solution.py:100
  410.7 1.1 gather.31
  411.8 7.6 %gather_fusion.2 = f32[2048,128]{1,0:T(8,128)} fusion(f32[256,128]{1,0:T(8,128)S(1)} %bitcast.112, s32[2048]{0:T(1024)S(1)} %copy-done.46), kind=kCustom, calls=%fused_computation.2 | custom fusion | bytes 2105344 | tf_op jit(solution)/shard_map/gather | solution.py:100
  419.4 2.4 gather.32
  421.8 6.4 %gather_fusion.3 = f32[2048,128]{1,0:T(8,128)S(1)} fusion(f32[256,128]{1,0:T(8,128)S(1)} %bitcast.111, s32[2048]{0:T(1024)} %broadcast_clamp_fusion.1), kind=kCustom, calls=%fused_computation.3 | custom fusion | bytes 2105344 | tf_op jit(solution)/shard_map/gather | solution.py:100
  428.2 1.3 gather.33
  429.5 7.6 %gather_fusion.4 = f32[2048,128]{1,0:T(8,128)} fusion(f32[256,128]{1,0:T(8,128)S(1)} %bitcast.110, s32[2048]{0:T(1024)S(1)} %copy-done.45), kind=kCustom, calls=%fused_computation.4 | custom fusion | bytes 2105344 | tf_op jit(solution)/shard_map/gather | solution.py:100
  437.2 2.5 gather.34
  439.8 3.5 subtract_convert_fusion
  443.6 0.2 fusion.88
  443.8 0.2 fusion.87
  444.1 0.2 fusion.86
  444.3 0.2 fusion.85
  444.6 0.2 convolution_add_fusion
  444.8 0.2 convolution_add_fusion.1
  445.1 0.2 convolution_add_fusion.2
  445.3 0.2 convolution_add_fusion.3
  445.6 0.2 convolution_add_fusion.4
  445.9 1.5 dynamic-slice_subtract_fusion
  447.4 0.6 mul.192
  448.0 0.6 mul.196
  448.7 0.6 mul.200
  449.3 0.6 mul.204
  449.9 0.6 mul.208
  450.7 2.3 clamp_subtract_fusion
  (122 shorter events, 1.3 us)
Async XLA Ops:
  7.2 2.9 copy-start
  7.2 2.9 copy-start.1
  7.2 2.9 copy-start.18
  7.2 99.7 %all-gather.2.cloned.1.call-start = ((), (), s32[]{:S(2)}) async-start(), calls=%async_computation.1 | async-start | bytes 8912896 | tf_op jit(solution)/shard_map/all_gather | solution.py:59
  7.9 241.6 %reduce-scatter.2.cloned.1.call-start = ((), (), s32[]{:S(2)}) async-start(), calls=%async_computation.2 | async-start | bytes 17825792 | tf_op jit(solution)/shard_map/reduce_scatter | solution.py:63
  10.1 96.8 %copy-start.49 = (f32[128]{0:T(128)}, f32[128]{0:T(128)S(1)}, u32[]{:S(2)}) copy-start(f32[128]{0:T(128)S(1)} %add_rsqrt_fusion) | copy-start | bytes 1540
  18.3 0.8 copy-start.26
  18.3 7.1 %copy-start.19 = (s32[5,2048]{1,0:T(8,128)S(1)}, s32[5,2048]{1,0:T(8,128)}, u32[]{:S(2)}) copy-start(s32[5,2048]{1,0:T(8,128)} %param.12) | copy-start | bytes 122884
  18.3 10.2 %copy-start.28 = (f32[1,5,2048]{2,0,1:T(1,128)S(1)}, f32[1,5,2048]{2,0,1:T(1,128)}, u32[]{:S(2)}) copy-start(f32[1,5,2048]{2,0,1:T(1,128)} %param.14) | copy-start | bytes 122884
  18.3 52.5 %copy-start.29 = (f32[1,5,2048]{2,0,1:T(1,128)S(1)}, f32[1,5,2048]{2,0,1:T(1,128)}, u32[]{:S(2)}) copy-start(f32[1,5,2048]{2,0,1:T(1,128)} %param.15) | copy-start | bytes 122884
  18.3 376.4 %all-reduce.2.cloned.1.call-start = ((), (), s32[]{:S(2)}) async-start(), calls=%async_computation.3 | async-start | bytes 1310720 | tf_op jit(solution)/shard_map/psum | solution.py:89
  25.4 228.4 %copy-start.32 = (bf16[2048]{0:T(1024)(128)(2,1)}, bf16[2048]{0:T(1024)(128)(2,1)S(1)}, u32[]{:S(2)}) copy-start(bf16[2048]{0:T(1024)(128)(2,1)S(1)} %get-tuple-element.12) | copy-start | bytes 12292
  25.4 229.2 %copy-start.30 = (bf16[2048]{0:T(1024)(128)(2,1)}, bf16[2048]{0:T(1024)(128)(2,1)S(1)}, u32[]{:S(2)}) copy-start(bf16[2048]{0:T(1024)(128)(2,1)S(1)} %get-tuple-element.13) | copy-start | bytes 12292
  25.4 230.1 %copy-start.34 = (bf16[2048]{0:T(1024)(128)(2,1)}, bf16[2048]{0:T(1024)(128)(2,1)S(1)}, u32[]{:S(2)}) copy-start(bf16[2048]{0:T(1024)(128)(2,1)S(1)} %get-tuple-element.11) | copy-start | bytes 12292
  25.4 231.0 %copy-start.36 = (bf16[2048]{0:T(1024)(128)(2,1)}, bf16[2048]{0:T(1024)(128)(2,1)S(1)}, u32[]{:S(2)}) copy-start(bf16[2048]{0:T(1024)(128)(2,1)S(1)} %get-tuple-element.10) | copy-start | bytes 12292
  25.4 231.8 %copy-start.38 = (bf16[2048]{0:T(1024)(128)(2,1)}, bf16[2048]{0:T(1024)(128)(2,1)S(1)}, u32[]{:S(2)}) copy-start(bf16[2048]{0:T(1024)(128)(2,1)S(1)} %get-tuple-element.9) | copy-start | bytes 12292
  106.8 148.7 %copy-start.20 = (s32[1,2048]{1,0:T(1,128)}, s32[1,2048]{1,0:T(1,128)S(1)}, u32[]{:S(2)}) copy-start(s32[1,2048]{1,0:T(1,128)S(1)} %get-tuple-element.38) | copy-start | bytes 24580
  106.8 149.6 %copy-start.22 = (s32[1,2048]{1,0:T(1,128)}, s32[1,2048]{1,0:T(1,128)S(1)}, u32[]{:S(2)}) copy-start(s32[1,2048]{1,0:T(1,128)S(1)} %get-tuple-element.41) | copy-start | bytes 24580
  106.8 150.4 %copy-start.24 = (s32[1,2048]{1,0:T(1,128)}, s32[1,2048]{1,0:T(1,128)S(1)}, u32[]{:S(2)}) copy-start(s32[1,2048]{1,0:T(1,128)S(1)} %get-tuple-element.37) | copy-start | bytes 24580
  257.8 0.8 copy-start.17
  258.7 136.1 %copy-start.10 = (f32[1,5,32768]{2,0,1:T(1,128)S(1)}, f32[1,5,32768]{2,0,1:T(1,128)}, u32[]{:S(2)}) copy-start(f32[1,5,32768]{2,0,1:T(1,128)} %all_gather.10) | copy-start | bytes 1966084
  258.7 136.1 %copy-start.11 = (f32[1,5,32768]{2,0,1:T(1,128)S(1)}, f32[1,5,32768]{2,0,1:T(1,128)}, u32[]{:S(2)}) copy-start(f32[1,5,32768]{2,0,1:T(1,128)} %all_gather.11) | copy-start | bytes 1966084
  263.2 135.1 %copy-start.48 = (s32[2048]{0:T(1024)S(1)}, s32[2048]{0:T(1024)}, u32[]{:S(2)}) copy-start(s32[2048]{0:T(1024)} %broadcast_clamp_fusion.4) | copy-start | bytes 24580
  398.2 5.8 %copy-start.9 = (f32[1,5,32768]{2,0,1:T(1,128)}, f32[1,5,32768]{2,0,1:T(1,128)S(1)}, u32[]{:S(2)}) copy-start(f32[1,5,32768]{2,0,1:T(1,128)S(1)} %get-tuple-element.16) | copy-start | bytes 1966084
  404.0 1.2 copy-start.47
  410.7 1.1 copy-start.46
  428.2 1.3 copy-start.3
  428.2 1.3 copy-start.45
  437.1 2.5 copy-start.2
  437.2 2.5 copy-start.40
  437.2 2.5 copy-start.41
  437.2 2.5 copy-start.42
  437.2 2.5 copy-start.43
  437.2 2.5 copy-start.44
  439.7 3.6 copy-start.25
  439.7 3.6 copy-start.27
  439.7 3.6 copy-start.39
  439.7 3.8 copy-start.23
  439.7 3.8 copy-start.37
  439.8 4.1 copy-start.21
  439.8 4.1 copy-start.35
  439.8 4.3 copy-start.33
  443.3 1.0 copy-start.31
  444.1 3.3 copy-start.12
  444.6 3.4 copy-start.13
  445.3 3.3 copy-start.14
  445.8 3.4 copy-start.15
  447.4 2.5 copy-start.16
  448.0 2.5 copy-start.7
  448.0 2.5 copy-start.8
  448.6 1.9 copy-start.4
  448.6 1.9 copy-start.5
  448.7 2.0 copy-start.6
Sparse Core Ops, SparseCore 0:
  10.8 85.1 all-gather.1
  100.5 148.9 reduce-scatter.1
  258.8 135.9 all-reduce.1
where the time goes:
time: 460 us; the launch traced here: 459 us
  waiting for transfers between devices  265 us (58%)
  blocking collectives  78.3 us (17%)
  local copies, waits for them, and re-layouts  53.3 us (12%)
  matrix products  24 us (5%)
  other arithmetic  23.9 us (5%)
  between operations  14.5 us (3%)
    reduce_scatter x1, waiting for transfers between devices, on_device(): lax.psum_scatter(lax.dot_general(inputs, key_cotangent, contract_first, p...  133 us
    psum x1, waiting for transfers between devices, on_device(): total = lax.psum(local_table, 'dp')  132 us
    all_gather x1, blocking collectives, on_device(): lax.all_gather(momentum, 'dp', axis=2, tiled=True)  42.3 us
    gather x10, local copies, waits for them, and re-layouts, on_device(): error_rows[row_index][bucket[row_index]] * sign_values[row_index][:, None]  41.2 us
    all_gather x1, blocking collectives, on_device(): lax.all_gather(error, 'dp', axis=2, tiled=True)  36 us
  transfers between devices with their start and end apart: 3, of which 2 were waited for; matrix products, arithmetic and copies ran while one was open for 7% of the time, Pallas kernels for 0%

commit v1 on v0

v1 whole, which is shorter than its diff:
```python
import functools
import math

import jax
import jax.numpy as jnp
from jax import lax
from jax.experimental import pallas as pl
from jax.experimental.pallas import tpu as pltpu
from jax.sharding import PartitionSpec as P

ROWS = 5
NBB = 256
BLOCK = 128
EPS = 1e-05
DECAY = 0.9
THRESHOLD = 1.0
N = 16
Z = 8
BF = jnp.bfloat16
F32 = jnp.float32
MESH = pl.DeviceIdType.MESH
PLAIN = (((1,), (0,)), ((), ()))
LAST = (((1,), (1,)), ((), ()))
FIRST = (((0,), (0,)), ((), ()))
DP_ORDER = [(1, d) for d in (4, 3, 5, 2, 6, 1, 7)] + [(0, d) for d in (4, 3, 5, 2, 6, 1, 7)] + [(1, 0)]


def dot(a, b, numbers):
    return lax.dot_general(a, b, numbers, preferred_element_type=F32)


def middle_three(first, second, third):
    return jnp.maximum(jnp.minimum(first, second), jnp.minimum(jnp.maximum(first, second), third))


def middle_five(items):
    upper_pair = jnp.minimum(jnp.maximum(items[0], items[1]), jnp.maximum(items[2], items[3]))
    lower_pair = jnp.maximum(jnp.minimum(items[0], items[1]), jnp.minimum(items[2], items[3]))
    return middle_three(items[4], upper_pair, lower_pair)


def split(values):
    upper = values.astype(BF)
    return upper, (values - upper.astype(F32)).astype(BF)


def kernel(
    scale,
    hs_hbm, gain_ref, kw_hbm, cot_hbm, bucket_ref, bits_ref, mom_ref, err_ref,
    grad_hbm, mom_out, err_out, upd_out,
    hs_v, hs_rx, cot_v, cot_rx, kw_v, ig_tx, ig_rx, acc, blk, blk2, sel, table, table_bf, rs_rx, e_all,
    e_mid, out_v, gcol, inv_v, ublk, ublk2,
    load_sem, out_sem, cot_tx_s, cot_fw_s, cot_s, hs_tx_s, hs_s, ig_tx_s, ig_s, rs_tx_s, rs_s, ag_tx_s, ag_s, misc_s,
):
    dp = lax.axis_index("dp")
    me = lax.axis_index("fsdp")
    xlo, z = dp // Z, dp % Z
    y, xhi, core = me // 4, (me // 2) % 2, me % 2
    tokens, width = hs_v.shape[1], hs_v.shape[2]

    def group_slot(dy, dx, dc):
        return ((y + dy) % 4) * 4 + ((xhi + dx) % 2) * 2 + (core + dc) % 2

    def group_peer(dy, dx, dc):
        return ((xlo + dx) % 2) * Z + z, group_slot(dy, dx, dc)

    def dp_peer(dx, dz):
        return ((xlo + dx) % 2) * Z + (z + dz) % Z

    offsets = [(i // 4, (i // 2) % 2, i % 2) for i in range(1, N)]

    hs_loads = [
        pltpu.make_async_copy(hs_hbm.at[:, pl.ds(s * width, width)], hs_v.at[s], load_sem.at[s]) for s in range(N)
    ]
    cot_load = pltpu.make_async_copy(cot_hbm, cot_v, misc_s.at[0])
    kw_load = pltpu.make_async_copy(kw_hbm, kw_v, misc_s.at[1])
    for copy in hs_loads:
        copy.start()
    cot_load.start()
    kw_load.start()

    barrier = pltpu.get_barrier_semaphore()
    for off in offsets:
        pl.semaphore_signal(barrier, inc=1, device_id=group_peer(*off), device_id_type=MESH)
    for off in DP_ORDER:
        pl.semaphore_signal(barrier, inc=1, device_id=(dp_peer(*off), me), device_id_type=MESH)

    squares = jnp.zeros((tokens, BLOCK), F32)
    for s in range(N):
        hs_loads[s].wait()
        part = hs_v[s].astype(F32)
        part = part * part
        for q in range(width // BLOCK):
            squares = squares + part[:, q * BLOCK:(q + 1) * BLOCK]
    inverse = lax.rsqrt(jnp.sum(squares, axis=1, keepdims=True) / (N * width) + EPS)
    inv_v[...] = jnp.broadcast_to(inverse, (tokens, BLOCK))
    cot_load.wait()
    cot_rx[me] = (cot_v[...].astype(F32) * inverse).astype(BF)

    pl.semaphore_wait(barrier, 2 * (N - 1))

    def cot_copy(off, sem):
        return pltpu.make_async_remote_copy(
            src_ref=cot_rx.at[me], dst_ref=cot_rx.at[me], send_sem=sem, recv_sem=cot_s.at[me],
            device_id=group_peer(*off), device_id_type=MESH)

    cot_sends = [
        cot_copy(off, cot_tx_s.at[k]) for k, off in enumerate(o for o in offsets if o[2] == 0 or o == (0, 0, 1))
    ]
    for copy in cot_sends:
        copy.start()

    def hs_copy(k, off):
        return pltpu.make_async_remote_copy(
            src_ref=hs_v.at[group_slot(*off)], dst_ref=hs_rx.at[me], send_sem=hs_tx_s.at[k], recv_sem=hs_s.at[me],
            device_id=group_peer(*off), device_id_type=MESH)

    hs_sends = [hs_copy(k, off) for k, off in enumerate(offsets)]
    for copy in hs_sends:
        copy.start()
    own = pltpu.make_async_copy(hs_v.at[me], hs_rx.at[me], misc_s.at[2])
    own.start()

    gain_row = gain_ref[:, pl.ds(pl.multiple_of(me * width, width), width)]
    gcol[...] = jnp.transpose(jnp.broadcast_to(gain_row * scale, (BLOCK, width)))

    for j in range(ROWS):
        ids = jnp.broadcast_to(bucket_ref[j:j + 1, :], (16, bucket_ref.shape[1]))
        signs = jnp.broadcast_to((2 * bits_ref[j:j + 1, :] - 1).astype(F32), (16, bucket_ref.shape[1]))
        row = lax.broadcasted_iota(jnp.int32, (16, bucket_ref.shape[1]), 0)

        def fill(i, carry, j=j, ids=ids, signs=signs, row=row):
            start = pl.multiple_of(i * 16, 16)
            sel[j, pl.ds(start, 16), :] = jnp.where(ids == row + i * 16, signs, 0.0).astype(BF)
            return carry

        lax.fori_loop(0, NBB // 16, fill, 0)
    acc[...] = jnp.zeros_like(acc)
    kw_load.wait()
    own.wait()

    def wait_slot(buffer, sem, slot):
        pltpu.make_async_remote_copy(
            src_ref=buffer.at[slot], dst_ref=buffer.at[slot], send_sem=misc_s.at[3], recv_sem=sem.at[slot],
            device_id=group_peer(0, 0, 1), device_id_type=MESH).wait_recv()

    def forward(i):
        slot = group_slot(4 - i // 2, i % 2, 0)
        return slot, pltpu.make_async_remote_copy(
            src_ref=cot_rx.at[slot], dst_ref=cot_rx.at[slot], send_sem=cot_fw_s.at[i], recv_sem=cot_s.at[slot],
            device_id=group_peer(0, 0, 1), device_id_type=MESH)

    for i in range(1, N // 2):
        slot, copy = forward(i)
        wait_slot(cot_rx, cot_s, slot)
        copy.start()

    def input_grad(i, carry):
        chip = ((y + 4 - i // 2) % 4) * 2 + (xhi + i) % 2
        other = chip * 2 + (core + 1) % 2
        wait_slot(cot_rx, cot_s, other)
        rows = cot_rx[pl.ds(chip * 2, 2)].reshape(2 * tokens, cot_rx.shape[2])
        product = dot(rows, kw_v[...], LAST).astype(BF)
        ig_tx[pl.ds(chip * 2, 2)] = product.reshape(2, tokens, width)
        return carry

    lax.fori_loop(0, N // 2, input_grad, 0)

    def accumulate(chip):
        rows = hs_rx[pl.ds(chip * 2, 2)].reshape(2 * tokens, width)
        cots = cot_rx[pl.ds(chip * 2, 2)].reshape(2 * tokens, cot_rx.shape[2])
        acc[...] += dot(rows, cots, FIRST)

    def chip_of(i):
        return ((y + 4 - i // 2) % 4) * 2 + (xhi + i) % 2

    def weight_grad(i, carry):
        chip = chip_of(i)
        wait_slot(hs_rx, hs_s, chip * 2 + (core + 1) % 2)

        @pl.when(i > 0)
        def _():
            wait_slot(hs_rx, hs_s, chip * 2 + core)

        accumulate(chip)
        return carry

    lax.fori_loop(0, N // 2, weight_grad, 0)

    ig_sends = [
        pltpu.make_async_remote_copy(
            src_ref=ig_tx.at[group_slot(*off)], dst_ref=ig_rx.at[me], send_sem=ig_tx_s.at[k], recv_sem=ig_s.at[me],
            device_id=group_peer(*off), device_id_type=MESH)
        for k, off in enumerate(offsets)
    ]
    for copy in ig_sends:
        copy.start()
    ig_own = pltpu.make_async_copy(ig_tx.at[me], ig_rx.at[me], misc_s.at[4])
    ig_own.start()

    parts = width // BLOCK
    for q in range(parts):
        blk[pl.ds(q, width, stride=parts), :] = acc[:, q * BLOCK:(q + 1) * BLOCK] * gcol[...]

    def to_halves(i, carry):
        rows = pl.ds(pl.multiple_of(i * 256, 256), 256)
        upper, lower = split(blk[rows, :])
        blk2[rows, 0:BLOCK] = upper
        blk2[rows, BLOCK:] = lower
        return carry

    lax.fori_loop(0, blk.shape[0] // 256, to_halves, 0)

    def sketch_row(j, carry):
        both = dot(sel[j], blk2[...], PLAIN)
        total = both[:, :BLOCK] + both[:, BLOCK:]
        table[j] = total
        table_bf[j] = total.astype(BF)
        return carry

    lax.fori_loop(0, ROWS, sketch_row, 0)

    share = NBB // N
    rs_sends = []
    for k, off in enumerate(DP_ORDER):
        target = dp_peer(*off)
        rs_sends.append(pltpu.make_async_remote_copy(
            src_ref=table_bf.at[:, pl.ds(pl.multiple_of(target * share, share), share), :], dst_ref=rs_rx.at[dp],
            send_sem=rs_tx_s.at[k], recv_sem=rs_s.at[dp], device_id=(target, me), device_id_type=MESH))
    for copy in rs_sends:
        copy.start()
    mine = pl.ds(pl.multiple_of(dp * share, share), share)
    for t in range(share):
        e_mid[0, :, t, :] = mom_ref[0, :, t * BLOCK:(t + 1) * BLOCK]
        e_mid[1, :, t, :] = err_ref[0, :, t * BLOCK:(t + 1) * BLOCK]
    total = table[:, mine, :]
    for off in DP_ORDER:
        source = dp_peer(*off)
        pltpu.make_async_remote_copy(
            src_ref=rs_rx.at[source], dst_ref=rs_rx.at[source], send_sem=misc_s.at[3], recv_sem=rs_s.at[source],
            device_id=(source, me), device_id_type=MESH).wait_recv()
        total = total + rs_rx[source].astype(F32)
    momentum_new = DECAY * e_mid[0] + total
    error_sum = e_mid[1] + momentum_new
    e_mid[0] = momentum_new
    e_mid[1] = error_sum
    e_all[:, mine, :] = error_sum.astype(BF)
    for t in range(share):
        mom_out[0, :, t * BLOCK:(t + 1) * BLOCK] = e_mid[0, :, t, :]
    ag_sends = []
    for k, off in enumerate(DP_ORDER):
        ag_sends.append(pltpu.make_async_remote_copy(
            src_ref=e_all.at[:, mine, :], dst_ref=e_all.at[:, mine, :], send_sem=ag_tx_s.at[k],
            recv_sem=ag_s.at[dp], device_id=(dp_peer(*off), me), device_id_type=MESH))
    for copy in ag_sends:
        copy.start()

    ig_own.wait()

    def row_sums(i, carry):
        chip = chip_of(i)
        wait_slot(ig_rx, ig_s, chip * 2 + (core + 1) % 2)

        @pl.when(i > 0)
        def _():
            wait_slot(ig_rx, ig_s, chip * 2 + core)

        for h in range(2):
            slot = chip * 2 + h
            gains = gain_ref[:, pl.ds(pl.multiple_of(slot * width, width), width)]
            product = ig_rx[slot].astype(F32) * hs_v[slot].astype(F32) * gains
            for q in range(parts):
                carry = carry + product[:, q * BLOCK:(q + 1) * BLOCK]
        return carry

    sums = lax.fori_loop(0, N // 2, row_sums, jnp.zeros((tokens, BLOCK), F32))
    mean_term = jnp.sum(sums, axis=1, keepdims=True) / (N * width)
    inverse = inv_v[:, 0:1]
    factor = inverse * inverse * mean_term

    def grad_copy(s):
        return pltpu.make_async_copy(
            out_v.at[s], grad_hbm.at[:, pl.ds(pl.multiple_of(s * width, width), width)], out_sem.at[s])

    def hidden(s, carry):
        gains = gain_ref[:, pl.ds(pl.multiple_of(s * width, width), width)]
        out_v[s] = (ig_rx[s].astype(F32) * gains - hs_v[s].astype(F32) * factor).astype(BF)
        grad_copy(s).start()
        return carry

    lax.fori_loop(0, N, hidden, 0)

    for off in DP_ORDER:
        source = dp_peer(*off)
        theirs = pl.ds(pl.multiple_of(source * share, share), share)
        pltpu.make_async_remote_copy(
            src_ref=e_all.at[:, theirs, :], dst_ref=e_all.at[:, theirs, :], send_sem=misc_s.at[3],
            recv_sem=ag_s.at[source], device_id=(source, me), device_id_type=MESH).wait_recv()

    def estimate(i, carry):
        start = pl.multiple_of(i * 512, 512)
        reads = [dot(e_all[j], sel[j, :, pl.ds(start, 512)], FIRST) for j in range(ROWS)]
        middle = middle_five(reads)
        update = jnp.transpose(middle - jnp.clip(middle, -THRESHOLD, THRESHOLD))
        rows = pl.ds(start, 512)
        ublk[rows, :] = update
        upper, lower = split(update)
        ublk2[rows, 0:BLOCK] = upper
        ublk2[rows, BLOCK:] = lower
        return carry

    lax.fori_loop(0, ublk.shape[0] // 512, estimate, 0)
    for q in range(parts):
        upd_out[:, q * BLOCK:(q + 1) * BLOCK] = ublk[pl.ds(q, width, stride=parts), :]
    selected = sel[:, mine, :].reshape(ROWS * share, sel.shape[2])
    both = dot(selected, ublk2[...], PLAIN)
    e_mid[1] = e_mid[1] - (both[:, :BLOCK] + both[:, BLOCK:]).reshape(ROWS, share, BLOCK)
    for t in range(share):
        err_out[0, :, t * BLOCK:(t + 1) * BLOCK] = e_mid[1, :, t, :]

    for copy in cot_sends + hs_sends + ig_sends + rs_sends + ag_sends:
        copy.wait_send()
    for i in range(1, N // 2):
        forward(i)[1].wait_send()
    for s in range(N):
        grad_copy(s).wait()


def on_device(hidden_states, gain, key_weight, key_cotangent, bucket, sign_bits, momentum, error):
    tokens, model = hidden_states.shape
    width, keys = key_weight.shape
    count = bucket.shape[1]
    scale = 1.0 / math.sqrt(tokens * N) / N
    any_spec = pl.BlockSpec(memory_space=pl.ANY)
    vmem = pl.BlockSpec(memory_space=pltpu.VMEM)
    dma = pltpu.SemaphoreType.DMA
    share = momentum.shape[2] // BLOCK
    return pl.pallas_call(
        functools.partial(kernel, scale),
        out_shape=(
            jax.ShapeDtypeStruct((tokens, model), BF),
            jax.ShapeDtypeStruct(momentum.shape, F32),
            jax.ShapeDtypeStruct(error.shape, F32),
            jax.ShapeDtypeStruct((width, keys), F32),
        ),
        in_specs=[any_spec, vmem, any_spec, any_spec, vmem, vmem, vmem, vmem],
        out_specs=(any_spec, vmem, vmem, vmem),
        scratch_shapes=[
            pltpu.VMEM((N, tokens, width), BF),
            pltpu.VMEM((N, tokens, width), BF),
            pltpu.VMEM((tokens, keys), BF),
            pltpu.VMEM((N, tokens, keys), BF),
            pltpu.VMEM((width, keys), BF),
            pltpu.VMEM((N, tokens, width), BF),
            pltpu.VMEM((N, tokens, width), BF),
            pltpu.VMEM((width, keys), F32),
            pltpu.VMEM((count, BLOCK), F32),
            pltpu.VMEM((count, 2 * BLOCK), BF),
            pltpu.VMEM((ROWS, NBB, count), BF),
            pltpu.VMEM((ROWS, NBB, BLOCK), F32),
            pltpu.VMEM((ROWS, NBB, BLOCK), BF),
            pltpu.VMEM((N, ROWS, share, BLOCK), BF),
            pltpu.VMEM((ROWS, NBB, BLOCK), BF),
            pltpu.VMEM((2, ROWS, share, BLOCK), F32),
            pltpu.VMEM((N, tokens, width), BF),
            pltpu.VMEM((width, BLOCK), F32),
            pltpu.VMEM((tokens, BLOCK), F32),
            pltpu.VMEM((count, BLOCK), F32),
            pltpu.VMEM((count, 2 * BLOCK), BF),
            dma((N,)), dma((N,)), dma((8,)), dma((8,)), dma((N,)), dma((N,)), dma((N,)), dma((N,)), dma((N,)),
            dma((N,)), dma((N,)), dma((N,)), dma((N,)), dma((8,)),
        ],
        compiler_params=pltpu.CompilerParams(
            collective_id=0, has_side_effects=True, vmem_limit_bytes=60 * 1024 * 1024),
        name="step",
    )(hidden_states, gain.reshape(1, model), key_weight, key_cotangent, bucket, sign_bits, momentum, error)


def solution(mesh):
    in_specs = (
        P(("dp", "fsdp"), None),
        P(),
        P("fsdp", None),
        P(("dp", "fsdp"), None),
        P(None, "fsdp"),
        P(None, "fsdp"),
        P("fsdp", None, "dp"),
        P("fsdp", None, "dp"),
    )
    out_specs = (
        P(("dp", "fsdp"), None),
        P("fsdp", None, "dp"),
        P("fsdp", None, "dp"),
        P("fsdp", None),
    )
    return jax.shard_map(
        on_device, mesh=mesh, in_specs=in_specs, out_specs=out_specs, check_vma=False
    )
```

time: 460 us -> 92.8 us (0.20)
  the two profiles are of different devices: /device:TPU:8 before, /device:TPU:1 now
where the time goes in v1:
time: 92.8 us; the launch traced here: 92.4 us
  Pallas kernels  81.7 us (88%)
  local copies, waits for them, and re-layouts  10 us (11%)
    pallas_call x1, Pallas kernels, on_device(): pl.pallas_call(functools.partial(kernel, scale), out_shape=(jax.ShapeDtyp...  81.7 us
    unnamed x6, local copies, waits for them, and re-layouts  7.01 us
    pallas_call x2, local copies, waits for them, and re-layouts, on_device(): pl.pallas_call(functools.partial(kernel, scale), out_shape=(jax.ShapeDtyp...  3 us

profile of v1, /device:TPU:1, one launch (start us, length us, event | category | flops | bytes accessed | tf_op | source)
XLA Modules:
  0.0 92.4 jit_solution(18186374731896762502)
XLA Ops:
  0.6 1.4 %copy.12.mom_ref = f32[1,5,2048]{2,1,0:T(8,128)} copy(f32[1,5,2048]{2,0,1:T(1,128)} %param.14) | data formatting | bytes 81920 | tf_op args[6]
  2.1 1.4 %copy.13.err_ref = f32[1,5,2048]{2,1,0:T(8,128)} copy(f32[1,5,2048]{2,0,1:T(1,128)} %param.15) | data formatting | bytes 81920 | tf_op args[7]
  3.5 81.7 %step.1 = (bf16[128,8192]{1,0:T(8,128)(2,1)}, f32[1,5,2048]{2,1,0:T(8,128)}, f32[1,5,2048]{2,1,0:T(8,128)}, f32[512,512]{1,0:T(8,128)}) custom-call(bf16[128,8192]{1,0:T(8,128)(2,1)} %hs_hbm.1, f32[1,8192]{1,0:T(1,128)} %bitcast.1, bf16[512,512]{1,0:T(8,128)(2,1)} %kw_hbm.1, bf16[128,512]{1,0:T(8,128)(2,1)} %cot_hbm.1, s32[5,2048]{1,0:T(8,128)} %bucket_ref.1, ...), custom_call_target="tpu_custom_call" | custom-call | tf_op jit(solution)/shard_map/step/pallas_call | solution.py:338
  85.2 1.5 %copy.14 = f32[1,5,2048]{2,0,1:T(1,128)} copy(f32[1,5,2048]{2,1,0:T(8,128)} %get-tuple-element.5) | data formatting | bytes 81920 | tf_op jit(solution)/shard_map/step/pallas_call | solution.py:338
  86.7 1.5 %copy.15 = f32[1,5,2048]{2,0,1:T(1,128)} copy(f32[1,5,2048]{2,1,0:T(8,128)} %get-tuple-element.6) | data formatting | bytes 81920 | tf_op jit(solution)/shard_map/step/pallas_call | solution.py:338
  88.2 0.0 copy-start
  88.2 3.2 %copy.18 = bf16[128,8192]{1,0:T(8,128)(2,1)} copy(bf16[128,8192]{1,0:T(8,128)(2,1)} %get-tuple-element.12) | data formatting | bytes 4194304
  91.4 0.0 copy-done
  91.4 1.0 %copy.19 = f32[512,512]{1,0:T(8,128)} copy(f32[512,512]{1,0:T(8,128)S(1)} %copy-done) | data formatting | bytes 2097152
Async XLA Ops:
  88.2 3.2 %copy-start = (f32[512,512]{1,0:T(8,128)S(1)}, f32[512,512]{1,0:T(8,128)}, u32[]{:S(2)}) copy-start(f32[512,512]{1,0:T(8,128)} %get-tuple-element.15) | copy-start | bytes 3145732

commit v2 on v1

v2 whole, which is shorter than its diff:
```python
import functools
import math

import jax
import jax.numpy as jnp
from jax import lax
from jax.experimental import pallas as pl
from jax.experimental.pallas import tpu as pltpu
from jax.sharding import PartitionSpec as P

ROWS = 5
NBB = 256
BLOCK = 128
EPS = 1e-05
DECAY = 0.9
THRESHOLD = 1.0
N = 16
BLK = 4
Z = 8
BF = jnp.bfloat16
F32 = jnp.float32
MESH = pl.DeviceIdType.MESH
PLAIN = (((1,), (0,)), ((), ()))
LAST = (((1,), (1,)), ((), ()))
FIRST = (((0,), (0,)), ((), ()))
DP_ORDER = [(1, d) for d in (4, 3, 5, 2, 6, 1, 7)] + [(0, d) for d in (4, 3, 5, 2, 6, 1, 7)] + [(1, 0)]


def dot(a, b, numbers):
    return lax.dot_general(a, b, numbers, preferred_element_type=F32)


def middle_three(first, second, third):
    return jnp.maximum(jnp.minimum(first, second), jnp.minimum(jnp.maximum(first, second), third))


def middle_five(items):
    upper_pair = jnp.minimum(jnp.maximum(items[0], items[1]), jnp.maximum(items[2], items[3]))
    lower_pair = jnp.maximum(jnp.minimum(items[0], items[1]), jnp.minimum(items[2], items[3]))
    return middle_three(items[4], upper_pair, lower_pair)


def split(values):
    upper = values.astype(BF)
    return upper, (values - upper.astype(F32)).astype(BF)


def kernel(
    scale,
    hs_hbm, gain_ref, kw_hbm, cot_hbm, bucket_ref, bits_ref, mom_ref, err_ref,
    grad_hbm, mom_out, err_out, upd_out,
    hs_v, hs_rx, cot_v, cot_rx, kw_v, ig_tx, ig_rx, acc, blk, blk2, sel, table_bf, rs_rx, e_all,
    e_mid, out_v, gcol, inv_v, ublk, ublk2, sel_h, bucket_h, bits_h,
    load_sem, out_sem, cot_tx_s, cot_s, hs_tx_s, hs_s, ig_tx_s, ig_s, rs_tx_s, rs_s, ag_tx_s, ag_s, misc_s,
    shared_tx_s, shared_s,
):
    dp = lax.axis_index("dp")
    me = lax.axis_index("fsdp")
    xlo, z = dp // Z, dp % Z
    y, xhi, core = me // 4, (me // 2) % 2, me % 2
    tokens, width = hs_v.shape[1], hs_v.shape[2]

    def other(value):
        return value + 1 - 2 * (value % 2)

    def pick(kind, first, second):
        return first + kind * (second - first)

    def block_chip(kind, p):
        bx, by = p // 2, p % 2
        return (
            xhi + bx * pick(kind, 1 - 2 * xhi, 0),
            xlo + bx * (1 - 2 * xlo),
            y + by * (pick(kind, other(y), 3 - y) - y),
        )

    def held_slab(hi, lo, yy, kind, j):
        held_y = pick(kind, 3 - yy, other(yy)) if j else yy
        return held_y * 4 + pick(kind, hi, 1 - lo if j else lo) * 2 + kind

    def device(hi, lo, yy, zz, kind):
        return lo * Z + zz, yy * 4 + hi * 2 + kind

    def target(dc, p):
        kind = (core + dc) % 2
        return device(*block_chip(kind, p), z, kind)

    def target_slab(dc, p, j):
        kind = (core + dc) % 2
        return held_slab(*block_chip(kind, p), kind, j)

    def source(dc, p):
        return device(*block_chip(core, p), z, (core + dc) % 2)

    def dp_peer(dx, dz):
        return ((xlo + dx) % 2) * Z + (z + dz) % Z

    held = [held_slab(xhi, xlo, y, core, j) for j in range(2)]
    own_slab = held[0] == me
    unit = [pick(core, xlo, xhi), pick(core, xlo, 1 - xhi)]
    my_index = [unit[j] * Z + z for j in range(2)]

    def holder(j, dx, dz):
        u, zz = (xlo + dx) % 2, (z + Z - dz) % Z
        yy = pick(core, 3 - y, other(y)) if j else y
        hi, lo = (1 - u, 1 - xhi) if j else (u, xhi)
        return u * Z + zz, device(pick(core, xhi, hi), pick(core, u, lo), yy, zz, core)

    def owner(j, dx, dz):
        share_index = ((unit[j] + dx) % 2) * Z + (z + dz) % Z
        return share_index, (share_index, held[j])

    partner = [owner(j, 0, 0)[1] for j in range(2)]
    offsets = [(dc, p) for p in range(BLK) for dc in range(2) if (dc, p) != (0, 0)]

    hs_loads = [
        pltpu.make_async_copy(hs_hbm.at[:, pl.ds(s * width, width)], hs_v.at[s], load_sem.at[s]) for s in range(N)
    ]
    cot_load = pltpu.make_async_copy(cot_hbm, cot_v, misc_s.at[0])
    for copy in hs_loads:
        copy.start()
    cot_load.start()

    barrier = pltpu.get_barrier_semaphore()
    ready = 0
    for dc, p in offsets:
        pl.semaphore_signal(barrier, inc=1, device_id=source(dc, p), device_id_type=MESH)
        ready += 1
        if dc == 1 and p > 0:
            pl.semaphore_signal(barrier, inc=1, device_id=target(dc, p), device_id_type=MESH)
            ready += 1
    for off in DP_ORDER:
        pl.semaphore_signal(barrier, inc=1, device_id=(dp_peer(off[0], Z - off[1]), me), device_id_type=MESH)
        for j in range(2):
            pl.semaphore_signal(barrier, inc=1, device_id=holder(j, *off)[1], device_id_type=MESH)
        ready += 3

    for j in range(2):
        pl.semaphore_signal(barrier, inc=1, device_id=partner[j], device_id_type=MESH)
        ready += 1

    squares = jnp.zeros((tokens, BLOCK), F32)
    for s in range(N):
        hs_loads[s].wait()
        part = hs_v[s].astype(F32)
        part = part * part
        for q in range(width // BLOCK):
            squares = squares + part[:, q * BLOCK:(q + 1) * BLOCK]
    inverse = lax.rsqrt(jnp.sum(squares, axis=1, keepdims=True) / (N * width) + EPS)
    inv_v[...] = jnp.broadcast_to(inverse, (tokens, BLOCK))
    cot_load.wait()
    cot_rx[core] = (cot_v[...].astype(F32) * inverse).astype(BF)

    pl.semaphore_wait(barrier, ready)

    def shared(j):
        return [(bucket_ref, bucket_h.at[j], 2 * j), (bits_ref, bits_h.at[j], 2 * j + 1), (kw_hbm, kw_v.at[j], 4 + j)]

    def to_partner(j, item):
        src, dst, k = item
        return pltpu.make_async_remote_copy(
            src_ref=src, dst_ref=dst, send_sem=shared_tx_s.at[k], recv_sem=shared_s.at[k],
            device_id=partner[j], device_id_type=MESH)

    def to_self(item):
        src, dst, k = item
        return pltpu.make_async_copy(src, dst, shared_s.at[k])

    def send_shared(pick_items):
        @pl.when(jnp.logical_not(own_slab))
        def _():
            for item in pick_items(shared(0)):
                to_partner(0, item).start()

        @pl.when(own_slab)
        def _():
            for item in pick_items(shared(0)):
                to_self(item).start()

        for item in pick_items(shared(1)):
            to_partner(1, item).start()

    send_shared(lambda items: items[:2])

    cot_sends = [
        pltpu.make_async_remote_copy(
            src_ref=cot_rx.at[core], dst_ref=cot_rx.at[2 * p + core], send_sem=cot_tx_s.at[k],
            recv_sem=cot_s.at[2 * p + core], device_id=target(dc, p), device_id_type=MESH)
        for k, (dc, p) in enumerate(offsets)
    ]
    for copy in cot_sends:
        copy.start()
    hs_sends = [
        pltpu.make_async_remote_copy(
            src_ref=hs_v.at[target_slab(dc, p, j)], dst_ref=hs_rx.at[j * 2 * BLK + 2 * p + core],
            send_sem=hs_tx_s.at[j * 2 * BLK + k],
            recv_sem=hs_s.at[j * 2 * BLK + 2 * p + core], device_id=target(dc, p), device_id_type=MESH)
        for j in range(2) for k, (dc, p) in enumerate(offsets)
    ]
    for copy in hs_sends:
        copy.start()
    own = [
        pltpu.make_async_copy(hs_v.at[held[j]], hs_rx.at[j * 2 * BLK + core], misc_s.at[1 + j]) for j in range(2)
    ]
    for copy in own:
        copy.start()
    send_shared(lambda items: items[2:])

    for j in range(2):
        gain_row = gain_ref[:, pl.ds(pl.multiple_of(held[j] * width, width), width)]
        gcol[j] = jnp.transpose(jnp.broadcast_to(gain_row * scale, (BLOCK, width)))

    def selectors(ids_ref, sign_ref, out):
        for j in range(ROWS):
            ids = jnp.broadcast_to(ids_ref[j:j + 1, :], (16, ids_ref.shape[1]))
            signs = jnp.broadcast_to((2 * sign_ref[j:j + 1, :] - 1).astype(F32), (16, ids_ref.shape[1]))
            row = lax.broadcasted_iota(jnp.int32, (16, ids_ref.shape[1]), 0)

            def fill(i, carry, j=j, ids=ids, signs=signs, row=row):
                start = pl.multiple_of(i * 16, 16)
                out[j, pl.ds(start, 16), :] = jnp.where(ids == row + i * 16, signs, 0.0).astype(BF)
                return carry

            lax.fori_loop(0, NBB // 16, fill, 0)

    acc[...] = jnp.zeros_like(acc)
    for j in range(2):
        for item in shared(j)[:2]:
            to_self(item).wait()
        selectors(bucket_h.at[j], bits_h.at[j], sel_h.at[j])
    selectors(bucket_ref, bits_ref, sel)
    for copy in own:
        copy.wait()

    def wait_slot(buffer, sem, slot):
        pltpu.make_async_remote_copy(
            src_ref=buffer.at[slot], dst_ref=buffer.at[slot], send_sem=misc_s.at[3], recv_sem=sem.at[slot],
            device_id=target(1, 0), device_id_type=MESH).wait_recv()

    parts = width // BLOCK
    share = NBB // N

    def half_weight_grad(j):
        def weight_grad(p, carry):
            if j == 0:
                wait_slot(cot_rx, cot_s, 2 * p + (core + 1) % 2)
            wait_slot(hs_rx, hs_s, j * 2 * BLK + 2 * p + (core + 1) % 2)

            @pl.when(p > 0)
            def _():
                if j == 0:
                    wait_slot(cot_rx, cot_s, 2 * p + core)
                wait_slot(hs_rx, hs_s, j * 2 * BLK + 2 * p + core)

            rows = hs_rx[pl.ds(j * 2 * BLK + p * 2, 2)].reshape(2 * tokens, width)
            cots = cot_rx[pl.ds(p * 2, 2)].reshape(2 * tokens, cot_rx.shape[2])
            acc[j] += dot(rows, cots, FIRST)
            return carry

        lax.fori_loop(0, BLK, weight_grad, 0)

        for q in range(parts):
            blk[pl.ds(q, width, stride=parts), :] = acc[j, :, q * BLOCK:(q + 1) * BLOCK] * gcol[j]

        def to_halves(i, carry):
            rows = pl.ds(pl.multiple_of(i * 256, 256), 256)
            upper, lower = split(blk[rows, :])
            blk2[rows, 0:BLOCK] = upper
            blk2[rows, BLOCK:] = lower
            return carry

        lax.fori_loop(0, blk.shape[0] // 256, to_halves, 0)

        def sketch_row(i, carry):
            both = dot(sel_h[j, i], blk2[...], PLAIN)
            table_bf[j, i] = (both[:, :BLOCK] + both[:, BLOCK:]).astype(BF)
            return carry

        lax.fori_loop(0, ROWS, sketch_row, 0)

    def share_copy(j, k, off):
        index, place = owner(j, *off)
        return pltpu.make_async_remote_copy(
            src_ref=table_bf.at[j, :, pl.ds(pl.multiple_of(index * share, share), share), :],
            dst_ref=rs_rx.at[j * N + my_index[j]], send_sem=rs_tx_s.at[j * N + k],
            recv_sem=rs_s.at[j * N + my_index[j]],
            device_id=place, device_id_type=MESH)

    def ig_copy(j, k, dc, p):
        return pltpu.make_async_remote_copy(
            src_ref=ig_tx.at[j * 2 * BLK + 2 * p + (core + dc) % 2], dst_ref=ig_rx.at[held[j]],
            send_sem=ig_tx_s.at[j * 2 * BLK + k],
            recv_sem=ig_s.at[held[j]], device_id=source(dc, p), device_id_type=MESH)

    ig_sends = [ig_copy(j, k, dc, p) for j in range(2) for k, (dc, p) in enumerate(offsets)]
    ig_own = [
        pltpu.make_async_copy(ig_tx.at[j * 2 * BLK + core], ig_rx.at[held[j]], misc_s.at[4 + j]) for j in range(2)
    ]

    def send_input_grad(j):
        to_self(shared(j)[2]).wait()

        def input_grad(p, carry):
            rows = cot_rx[pl.ds(p * 2, 2)].reshape(2 * tokens, cot_rx.shape[2])
            product = dot(rows, kw_v[j], LAST).astype(BF)
            ig_tx[pl.ds(j * 2 * BLK + p * 2, 2)] = product.reshape(2, tokens, width)
            return carry

        lax.fori_loop(0, BLK, input_grad, 0)
        for k, (dc, p) in enumerate(offsets):
            ig_copy(j, k, dc, p).start()
        pltpu.make_async_copy(ig_tx.at[j * 2 * BLK + core], ig_rx.at[held[j]], misc_s.at[4 + j]).start()

    rs_sends = []
    for j in range(2):
        half_weight_grad(j)
        sends = [share_copy(j, k, off) for k, off in enumerate(DP_ORDER)]
        for copy in sends:
            copy.start()
        rs_sends += sends
        if j == 1:
            rs_sends.append(share_copy(1, N - 1, (0, 0)))
            rs_sends[-1].start()
        else:
            @pl.when(jnp.logical_not(own_slab))
            def _():
                share_copy(0, N - 1, (0, 0)).start()

            @pl.when(own_slab)
            def _():
                pltpu.make_async_copy(
                    table_bf.at[0, :, pl.ds(pl.multiple_of(my_index[0] * share, share), share), :],
                    rs_rx.at[my_index[0]], rs_s.at[my_index[0]]).start()
                send_input_grad(0)

    for j in range(2):
        if j == 0:
            pl.when(jnp.logical_not(own_slab))(lambda: send_input_grad(0))
        else:
            send_input_grad(1)

    mine = pl.ds(pl.multiple_of(dp * share, share), share)
    total = jnp.zeros((ROWS, share, BLOCK), F32)
    for j in range(2):
        for off in DP_ORDER + [(0, 0)]:
            index = j * N + holder(j, *off)[0]
            pltpu.make_async_copy(rs_rx.at[index], rs_rx.at[index], rs_s.at[index]).wait()
            total = total + rs_rx[index].astype(F32)
    momentum_new = DECAY * mom_ref[...] + total
    error_sum = err_ref[...] + momentum_new
    mom_out[...] = momentum_new
    e_mid[...] = error_sum
    e_all[:, mine, :] = error_sum.astype(BF)
    ag_sends = []
    for k, off in enumerate(DP_ORDER):
        ag_sends.append(pltpu.make_async_remote_copy(
            src_ref=e_all.at[:, mine, :], dst_ref=e_all.at[:, mine, :], send_sem=ag_tx_s.at[k],
            recv_sem=ag_s.at[dp], device_id=(dp_peer(*off), me), device_id_type=MESH))
    for copy in ag_sends:
        copy.start()

    for off in DP_ORDER:
        index = dp_peer(*off)
        theirs = pl.ds(pl.multiple_of(index * share, share), share)
        pltpu.make_async_remote_copy(
            src_ref=e_all.at[:, theirs, :], dst_ref=e_all.at[:, theirs, :], send_sem=misc_s.at[3],
            recv_sem=ag_s.at[index], device_id=(index, me), device_id_type=MESH).wait_recv()

    def estimate(i, carry):
        start = pl.multiple_of(i * 512, 512)
        reads = [dot(e_all[j], sel[j, :, pl.ds(start, 512)], FIRST) for j in range(ROWS)]
        middle = middle_five(reads)
        update = jnp.transpose(middle - jnp.clip(middle, -THRESHOLD, THRESHOLD))
        rows = pl.ds(start, 512)
        ublk[rows, :] = update
        upper, lower = split(update)
        ublk2[rows, 0:BLOCK] = upper
        ublk2[rows, BLOCK:] = lower
        return carry

    lax.fori_loop(0, ublk.shape[0] // 512, estimate, 0)
    for q in range(parts):
        upd_out[:, q * BLOCK:(q + 1) * BLOCK] = ublk[pl.ds(q, width, stride=parts), :]
    selected = sel[:, mine, :].reshape(ROWS * share, sel.shape[2])
    both = dot(selected, ublk2[...], PLAIN)
    err_out[...] = e_mid[...] - (both[:, :BLOCK] + both[:, BLOCK:]).reshape(ROWS, share, BLOCK)

    for copy in ig_own:
        copy.wait()

    def row_sums(p, carry):
        for j in range(2):
            for dc in range(2):
                slot = target_slab(dc, p, j)
                if dc == 1:
                    wait_slot(ig_rx, ig_s, slot)
                else:
                    @pl.when(p > 0)
                    def _(slot=slot):
                        wait_slot(ig_rx, ig_s, slot)

                gains = gain_ref[:, pl.ds(pl.multiple_of(slot * width, width), width)]
                product = ig_rx[slot].astype(F32) * hs_v[slot].astype(F32) * gains
                for q in range(parts):
                    carry = carry + product[:, q * BLOCK:(q + 1) * BLOCK]
        return carry

    sums = lax.fori_loop(0, BLK, row_sums, jnp.zeros((tokens, BLOCK), F32))
    mean_term = jnp.sum(sums, axis=1, keepdims=True) / (N * width)
    inverse = inv_v[:, 0:1]
    factor = inverse * inverse * mean_term

    def grad_copy(s):
        return pltpu.make_async_copy(
            out_v.at[s], grad_hbm.at[:, pl.ds(pl.multiple_of(s * width, width), width)], out_sem.at[s])

    def hidden(s, carry):
        gains = gain_ref[:, pl.ds(pl.multiple_of(s * width, width), width)]
        out_v[s] = (ig_rx[s].astype(F32) * gains - hs_v[s].astype(F32) * factor).astype(BF)
        grad_copy(s).start()
        return carry

    lax.fori_loop(0, N, hidden, 0)

    for copy in cot_sends + hs_sends + ig_sends + rs_sends + ag_sends:
        copy.wait_send()

    for item in shared(1):
        to_partner(1, item).wait_send()

    @pl.when(jnp.logical_not(own_slab))
    def _():
        for item in shared(0):
            to_partner(0, item).wait_send()
        share_copy(0, N - 1, (0, 0)).wait_send()

    for s in range(N):
        grad_copy(s).wait()


def on_device(hidden_states, gain, key_weight, key_cotangent, bucket, sign_bits, momentum, error):
    tokens, model = hidden_states.shape
    width, keys = key_weight.shape
    count = bucket.shape[1]
    scale = 1.0 / math.sqrt(tokens * N) / N
    any_spec = pl.BlockSpec(memory_space=pl.ANY)
    vmem = pl.BlockSpec(memory_space=pltpu.VMEM)
    dma = pltpu.SemaphoreType.DMA
    share = momentum.shape[2] // BLOCK
    flat = (ROWS, share, BLOCK)
    grad, momentum_new, error_new, update = pl.pallas_call(
        functools.partial(kernel, scale),
        out_shape=(
            jax.ShapeDtypeStruct((tokens, model), BF),
            jax.ShapeDtypeStruct((ROWS, share, BLOCK), F32),
            jax.ShapeDtypeStruct((ROWS, share, BLOCK), F32),
            jax.ShapeDtypeStruct((width, keys), F32),
        ),
        in_specs=[any_spec, vmem, any_spec, any_spec, vmem, vmem, vmem, vmem],
        out_specs=(any_spec, vmem, vmem, vmem),
        scratch_shapes=[
            pltpu.VMEM((N, tokens, width), BF),
            pltpu.VMEM((N, tokens, width), BF),
            pltpu.VMEM((tokens, keys), BF),
            pltpu.VMEM((2 * BLK, tokens, keys), BF),
            pltpu.VMEM((2, width, keys), BF),
            pltpu.VMEM((N, tokens, width), BF),
            pltpu.VMEM((N, tokens, width), BF),
            pltpu.VMEM((2, width, keys), F32),
            pltpu.VMEM((count, BLOCK), F32),
            pltpu.VMEM((count, 2 * BLOCK), BF),
            pltpu.VMEM((ROWS, NBB, count), BF),
            pltpu.VMEM((2, ROWS, NBB, BLOCK), BF),
            pltpu.VMEM((2 * N, ROWS, share, BLOCK), BF),
            pltpu.VMEM((ROWS, NBB, BLOCK), BF),
            pltpu.VMEM((ROWS, share, BLOCK), F32),
            pltpu.VMEM((N, tokens, width), BF),
            pltpu.VMEM((2, width, BLOCK), F32),
            pltpu.VMEM((tokens, BLOCK), F32),
            pltpu.VMEM((count, BLOCK), F32),
            pltpu.VMEM((count, 2 * BLOCK), BF),
            pltpu.VMEM((2, ROWS, NBB, count), BF),
            pltpu.VMEM((2,) + bucket.shape, jnp.int32),
            pltpu.VMEM((2,) + bucket.shape, jnp.int32),
            dma((N,)), dma((N,)), dma((8,)), dma((8,)), dma((N,)), dma((N,)), dma((N,)), dma((N,)),
            dma((2 * N,)), dma((2 * N,)), dma((N,)), dma((N,)), dma((8,)), dma((8,)), dma((8,)),
        ],
        compiler_params=pltpu.CompilerParams(
            collective_id=0, has_side_effects=True, vmem_limit_bytes=60 * 1024 * 1024),
        name="step",
    )(hidden_states, gain.reshape(1, model), key_weight, key_cotangent, bucket, sign_bits, momentum.reshape(flat), error.reshape(flat))
    return grad, momentum_new.reshape(momentum.shape), error_new.reshape(error.shape), update


def solution(mesh):
    in_specs = (
        P(("dp", "fsdp"), None),
        P(),
        P("fsdp", None),
        P(("dp", "fsdp"), None),
        P(None, "fsdp"),
        P(None, "fsdp"),
        P("fsdp", None, "dp"),
        P("fsdp", None, "dp"),
    )
    out_specs = (
        P(("dp", "fsdp"), None),
        P("fsdp", None, "dp"),
        P("fsdp", None, "dp"),
        P("fsdp", None),
    )
    return jax.shard_map(
        on_device, mesh=mesh, in_specs=in_specs, out_specs=out_specs, check_vma=False
    )
```

time: 92.8 us -> 75.4 us (0.81)
  Pallas kernels: 81.7 us -> 69.1 us
  local copies, waits for them, and re-layouts: 10 us -> 5.4 us
    pallas_call x1, Pallas kernels: 81.7 us -> 69.1 us  [on_device(): pl.pallas_call(functools.partial(kernel, scale), out_shape=(jax.ShapeDtyp...]
    pallas_call x2 -> x0, local copies, waits for them, and re-layouts: 3 us -> none  [on_device(): pl.pallas_call(functools.partial(kernel, scale), out_shape=(jax.ShapeDtyp...]
    unnamed x6 -> x10, local copies, waits for them, and re-layouts: 7.01 us -> 5.4 us
where the time goes in v2:
time: 75.4 us; the launch traced here: 75.2 us
  Pallas kernels  69.1 us (92%)
  local copies, waits for them, and re-layouts  5.4 us (7%)
    pallas_call x1, Pallas kernels, on_device(): pl.pallas_call(functools.partial(kernel, scale), out_shape=(jax.ShapeDtyp...  69.1 us
    unnamed x10, local copies, waits for them, and re-layouts  5.4 us

profile of v2, /device:TPU:1, one launch (start us, length us, event | category | flops | bytes accessed | tf_op | source)
XLA Modules:
  0.0 75.2 jit_solution(744710016982708487)
XLA Ops:
  0.6 69.1 %step.1 = (bf16[128,8192]{1,0:T(8,128)(2,1)}, f32[5,16,128]{2,1,0:T(8,128)}, f32[5,16,128]{2,1,0:T(8,128)}, f32[512,512]{1,0:T(8,128)}) custom-call(bf16[128,8192]{1,0:T(8,128)(2,1)} %hs_hbm.1, f32[1,8192]{1,0:T(1,128)} %bitcast.9, bf16[512,512]{1,0:T(8,128)(2,1)} %kw_hbm.1, bf16[128,512]{1,0:T(8,128)(2,1)} %cot_hbm.1, s32[5,2048]{1,0:T(8,128)} %bucket_ref.1, ...), custom_call_target="tpu_custom_call" | custom-call | tf_op jit(solution)/shard_map/step/pallas_call | solution.py:451
  69.8 0.0 copy-start.2
  69.8 0.0 copy-start.1
  69.8 0.0 copy-start
  69.8 3.2 %copy.20 = bf16[128,8192]{1,0:T(8,128)(2,1)} copy(bf16[128,8192]{1,0:T(8,128)(2,1)} %get-tuple-element.24) | data formatting | bytes 4194304
  73.0 0.0 copy-done.2
  73.0 0.6 copy.21
  73.6 0.0 copy-done.1
  73.6 0.6 copy.22
  74.2 0.0 copy-done
  74.2 1.0 %copy.23 = f32[512,512]{1,0:T(8,128)} copy(f32[512,512]{1,0:T(8,128)S(1)} %copy-done) | data formatting | bytes 2097152
Async XLA Ops:
  69.8 3.2 %copy-start.2 = (f32[5,16,128]{2,1,0:T(8,128)S(1)}, f32[5,16,128]{2,1,0:T(8,128)}, u32[]{:S(2)}) copy-start(f32[5,16,128]{2,1,0:T(8,128)} %get-tuple-element.9) | copy-start | bytes 122884
  69.8 3.8 %copy-start.1 = (f32[5,16,128]{2,1,0:T(8,128)S(1)}, f32[5,16,128]{2,1,0:T(8,128)}, u32[]{:S(2)}) copy-start(f32[5,16,128]{2,1,0:T(8,128)} %get-tuple-element.10) | copy-start | bytes 122884
  69.8 4.4 %copy-start = (f32[512,512]{1,0:T(8,128)S(1)}, f32[512,512]{1,0:T(8,128)}, u32[]{:S(2)}) copy-start(f32[512,512]{1,0:T(8,128)} %get-tuple-element.27) | copy-start | bytes 3145732

commit v3 on v2

--- a/solution.py
+++ b/solution.py
@@ -23,7 +23,7 @@
 PLAIN = (((1,), (0,)), ((), ()))
 LAST = (((1,), (1,)), ((), ()))
 FIRST = (((0,), (0,)), ((), ()))
-DP_ORDER = [(1, d) for d in (4, 3, 5, 2, 6, 1, 7)] + [(0, d) for d in (4, 3, 5, 2, 6, 1, 7)] + [(1, 0)]
+DP_ORDER = [(1, d) for d in (4, 3, 5, 2, 6, 1, 7, 0)] + [(0, d) for d in (4, 3, 5, 2, 6, 1, 7)]
 
 
 def dot(a, b, numbers):
@@ -47,12 +47,13 @@
 
 def kernel(
     scale,
-    hs_hbm, gain_ref, kw_hbm, cot_hbm, bucket_ref, bits_ref, mom_ref, err_ref,
-    grad_hbm, mom_out, err_out, upd_out,
+    hs_hbm, gain_hbm, kw_hbm, cot_hbm, bucket_hbm, bits_hbm, mom_hbm, err_hbm,
+    ig_hbm, mom_out, err_out, upd_hbm, fac_out,
     hs_v, hs_rx, cot_v, cot_rx, kw_v, ig_tx, ig_rx, acc, blk, blk2, sel, table_bf, rs_rx, e_all,
-    e_mid, out_v, gcol, inv_v, ublk, ublk2, sel_h, bucket_h, bits_h,
+    e_mid, upd_v, gcol, inv_v, ublk, ublk2, sel_h, bucket_h, bits_h,
+    gain_ref, bucket_ref, bits_ref, mom_ref, err_ref, mom_new, err_new, fac_v,
     load_sem, out_sem, cot_tx_s, cot_s, hs_tx_s, hs_s, ig_tx_s, ig_s, rs_tx_s, rs_s, ag_tx_s, ag_s, misc_s,
-    shared_tx_s, shared_s,
+    shared_tx_s, shared_s, small_s,
 ):
     dp = lax.axis_index("dp")
     me = lax.axis_index("fsdp")
@@ -117,9 +118,13 @@
         pltpu.make_async_copy(hs_hbm.at[:, pl.ds(s * width, width)], hs_v.at[s], load_sem.at[s]) for s in range(N)
     ]
     cot_load = pltpu.make_async_copy(cot_hbm, cot_v, misc_s.at[0])
+    pairs = [(gain_hbm, gain_ref), (bucket_hbm, bucket_ref), (bits_hbm, bits_ref), (mom_hbm, mom_ref), (err_hbm, err_ref)]
+    small_loads = [pltpu.make_async_copy(src, dst, small_s.at[k]) for k, (src, dst) in enumerate(pairs)]
     for copy in hs_loads:
         copy.start()
     cot_load.start()
+    for copy in small_loads:
+        copy.start()
 
     barrier = pltpu.get_barrier_semaphore()
     ready = 0
@@ -151,6 +156,8 @@
     cot_load.wait()
     cot_rx[core] = (cot_v[...].astype(F32) * inverse).astype(BF)
 
+    for copy in small_loads:
+        copy.wait()
     pl.semaphore_wait(barrier, ready)
 
     def shared(j):
@@ -271,9 +278,12 @@
 
         lax.fori_loop(0, blk.shape[0] // 256, to_halves, 0)
 
+    def half_sketch(j, dx):
+        rows = pl.ds(pl.multiple_of(((unit[j] + dx) % 2) * (NBB // 2), NBB // 2), NBB // 2)
+
         def sketch_row(i, carry):
-            both = dot(sel_h[j, i], blk2[...], PLAIN)
-            table_bf[j, i] = (both[:, :BLOCK] + both[:, BLOCK:]).astype(BF)
+            both = dot(sel_h[j, i, rows, :], blk2[...], PLAIN)
+            table_bf[j, i, rows, :] = (both[:, :BLOCK] + both[:, BLOCK:]).astype(BF)
             return carry
 
         lax.fori_loop(0, ROWS, sketch_row, 0)
@@ -314,10 +324,12 @@
     rs_sends = []
     for j in range(2):
         half_weight_grad(j)
-        sends = [share_copy(j, k, off) for k, off in enumerate(DP_ORDER)]
-        for copy in sends:
-            copy.start()
-        rs_sends += sends
+        for dx in (1, 0):
+            half_sketch(j, dx)
+            sends = [share_copy(j, k, off) for k, off in enumerate(DP_ORDER) if off[0] == dx]
+            for copy in sends:
+                copy.start()
+            rs_sends += sends
         if j == 1:
             rs_sends.append(share_copy(1, N - 1, (0, 0)))
             rs_sends[-1].start()
@@ -348,7 +360,9 @@
             total = total + rs_rx[index].astype(F32)
     momentum_new = DECAY * mom_ref[...] + total
     error_sum = err_ref[...] + momentum_new
-    mom_out[...] = momentum_new
+    mom_new[...] = momentum_new
+    out_copies = [pltpu.make_async_copy(mom_new, mom_out, small_s.at[5])]
+    out_copies[0].start()
     e_mid[...] = error_sum
     e_all[:, mine, :] = error_sum.astype(BF)
     ag_sends = []
@@ -358,6 +372,37 @@
             recv_sem=ag_s.at[dp], device_id=(dp_peer(*off), me), device_id_type=MESH))
     for copy in ag_sends:
         copy.start()
+
+    for copy in ig_own:
+        copy.wait()
+
+    def ig_store(slot):
+        return pltpu.make_async_copy(ig_rx.at[slot], ig_hbm.at[slot], out_sem.at[slot])
+
+    def row_sums(p, carry):
+        for j in range(2):
+            for dc in range(2):
+                slot = target_slab(dc, p, j)
+                if dc == 1:
+                    wait_slot(ig_rx, ig_s, slot)
+                else:
+                    @pl.when(p > 0)
+                    def _(slot=slot):
+                        wait_slot(ig_rx, ig_s, slot)
+
+                ig_store(slot).start()
+                gains = gain_ref[:, pl.ds(pl.multiple_of(slot * width, width), width)]
+                product = ig_rx[slot].astype(F32) * hs_v[slot].astype(F32) * gains
+                for q in range(parts):
+                    carry = carry + product[:, q * BLOCK:(q + 1) * BLOCK]
+        return carry
+
+    sums = lax.fori_loop(0, BLK, row_sums, jnp.zeros((tokens, BLOCK), F32))
+    mean_term = jnp.sum(sums, axis=1, keepdims=True) / (N * width)
+    inverse = inv_v[...]
+    fac_v[...] = inverse * inverse * mean_term
+    out_copies.append(pltpu.make_async_copy(fac_v, fac_out, small_s.at[7]))
+    out_copies[-1].start()
 
     for off in DP_ORDER:
         index = dp_peer(*off)
@@ -380,47 +425,15 @@
 
     lax.fori_loop(0, ublk.shape[0] // 512, estimate, 0)
     for q in range(parts):
-        upd_out[:, q * BLOCK:(q + 1) * BLOCK] = ublk[pl.ds(q, width, stride=parts), :]
+        upd_v[:, q * BLOCK:(q + 1) * BLOCK] = ublk[pl.ds(q, width, stride=parts), :]
+    upd_store = pltpu.make_async_copy(upd_v, upd_hbm, misc_s.at[6])
+    upd_store.start()
     selected = sel[:, mine, :].reshape(ROWS * share, sel.shape[2])
     both = dot(selected, ublk2[...], PLAIN)
-    err_out[...] = e_mid[...] - (both[:, :BLOCK] + both[:, BLOCK:]).reshape(ROWS, share, BLOCK)
-
-    for copy in ig_own:
-        copy.wait()
-
-    def row_sums(p, carry):
-        for j in range(2):
-            for dc in range(2):
-                slot = target_slab(dc, p, j)
-                if dc == 1:
-                    wait_slot(ig_rx, ig_s, slot)
-                else:
-                    @pl.when(p > 0)
-                    def _(slot=slot):
-                        wait_slot(ig_rx, ig_s, slot)
-
-                gains = gain_ref[:, pl.ds(pl.multiple_of(slot * width, width), width)]
-                product = ig_rx[slot].astype(F32) * hs_v[slot].astype(F32) * gains
-                for q in range(parts):
-                    carry = carry + product[:, q * BLOCK:(q + 1) * BLOCK]
-        return carry
-
-    sums = lax.fori_loop(0, BLK, row_sums, jnp.zeros((tokens, BLOCK), F32))
-    mean_term = jnp.sum(sums, axis=1, keepdims=True) / (N * width)
-    inverse = inv_v[:, 0:1]
-    factor = inverse * inverse * mean_term
-
-    def grad_copy(s):
-        return pltpu.make_async_copy(
-            out_v.at[s], grad_hbm.at[:, pl.ds(pl.multiple_of(s * width, width), width)], out_sem.at[s])
-
-    def hidden(s, carry):
-        gains = gain_ref[:, pl.ds(pl.multiple_of(s * width, width), width)]
-        out_v[s] = (ig_rx[s].astype(F32) * gains - hs_v[s].astype(F32) * factor).astype(BF)
-        grad_copy(s).start()
-        return carry
-
-    lax.fori_loop(0, N, hidden, 0)
+    err_new[...] = e_mid[...] - (both[:, :BLOCK] + both[:, BLOCK:]).reshape(ROWS, share, BLOCK)
+
+    out_copies.append(pltpu.make_async_copy(err_new, err_out, small_s.at[6]))
+    out_copies[-1].start()
 
     for copy in cot_sends + hs_sends + ig_sends + rs_sends + ag_sends:
         copy.wait_send()
@@ -434,8 +447,72 @@
             to_partner(0, item).wait_send()
         share_copy(0, N - 1, (0, 0)).wait_send()
 
-    for s in range(N):
-        grad_copy(s).wait()
+    for slot in range(N):
+        ig_store(slot).wait()
+    upd_store.wait()
+    for copy in out_copies:
+        copy.wait()
+
+
+def results_kernel(
+    ig_hbm, hs_hbm, gain_hbm, fac_hbm, mom_hbm, err_hbm, upd_hbm,
+    grad_hbm, mom_out, err_out, upd_out,
+    ig_v, hs_v, out_v, gain_v, fac_v, mom_v, err_v, upd_v, in_sem, hs_sem, out_sem, pass_in, pass_out,
+):
+    count = in_sem.shape[0]
+    height = hs_v.shape[0] // count
+    width = ig_v.shape[2]
+
+    def band(s):
+        return pl.ds(pl.multiple_of(s * height, height), height)
+
+    def load(s):
+        return (
+            pltpu.make_async_copy(ig_hbm.at[:, band(s), :], ig_v.at[:, band(s), :], in_sem.at[s]),
+            pltpu.make_async_copy(hs_hbm.at[band(s)], hs_v.at[band(s)], hs_sem.at[s]),
+        )
+
+    def store(s):
+        return pltpu.make_async_copy(out_v.at[band(s)], grad_hbm.at[band(s)], out_sem.at[s])
+
+    small = [
+        pltpu.make_async_copy(gain_hbm, gain_v, pass_in.at[3]), pltpu.make_async_copy(fac_hbm, fac_v, pass_in.at[4])
+    ]
+    for copy in small:
+        copy.start()
+    for s in range(count):
+        for copy in load(s):
+            copy.start()
+    passed = [(mom_hbm, mom_v, mom_out), (err_hbm, err_v, err_out), (upd_hbm, upd_v, upd_out)]
+    arrivals = [pltpu.make_async_copy(src, mid, pass_in.at[k]) for k, (src, mid, _) in enumerate(passed)]
+    departures = [pltpu.make_async_copy(mid, dst, pass_out.at[k]) for k, (_, mid, dst) in enumerate(passed)]
+    for copy in arrivals:
+        copy.start()
+    for copy in small:
+        copy.wait()
+
+    def hidden(s, carry):
+        for copy in load(s):
+            copy.wait()
+        factor = fac_v[band(s), :]
+        for t in range(N):
+            for q in range(width // BLOCK):
+                inner = slice(q * BLOCK, (q + 1) * BLOCK)
+                outer = slice(t * width + q * BLOCK, t * width + (q + 1) * BLOCK)
+                out_v[band(s), outer] = (
+                    ig_v[t, band(s), inner].astype(F32) * gain_v[:, outer] - hs_v[band(s), outer].astype(F32) * factor
+                ).astype(BF)
+        store(s).start()
+        return carry
+
+    lax.fori_loop(0, count, hidden, 0)
+    for arrival, departure in zip(arrivals, departures):
+        arrival.wait()
+        departure.start()
+    for s in range(count):
+        store(s).wait()
+    for departure in departures:
+        departure.wait()
 
 
 def on_device(hidden_states, gain, key_weight, key_cotangent, bucket, sign_bits, momentum, error):
@@ -444,20 +521,21 @@
     count = bucket.shape[1]
     scale = 1.0 / math.sqrt(tokens * N) / N
     any_spec = pl.BlockSpec(memory_space=pl.ANY)
-    vmem = pl.BlockSpec(memory_space=pltpu.VMEM)
     dma = pltpu.SemaphoreType.DMA
     share = momentum.shape[2] // BLOCK
     flat = (ROWS, share, BLOCK)
-    grad, momentum_new, error_new, update = pl.pallas_call(
+    gain_row = gain.reshape(1, model)
+    returned, momentum_new, error_new, update, factor = pl.pallas_call(
         functools.partial(kernel, scale),
         out_shape=(
-            jax.ShapeDtypeStruct((tokens, model), BF),
+            jax.ShapeDtypeStruct((N, tokens, width), BF),
             jax.ShapeDtypeStruct((ROWS, share, BLOCK), F32),
             jax.ShapeDtypeStruct((ROWS, share, BLOCK), F32),
             jax.ShapeDtypeStruct((width, keys), F32),
+            jax.ShapeDtypeStruct((tokens, BLOCK), F32),
         ),
-        in_specs=[any_spec, vmem, any_spec, any_spec, vmem, vmem, vmem, vmem],
-        out_specs=(any_spec, vmem, vmem, vmem),
+        in_specs=[any_spec] * 8,
+        out_specs=(any_spec,) * 5,
         scratch_shapes=[
             pltpu.VMEM((N, tokens, width), BF),
             pltpu.VMEM((N, tokens, width), BF),
@@ -474,7 +552,7 @@
             pltpu.VMEM((2 * N, ROWS, share, BLOCK), BF),
             pltpu.VMEM((ROWS, NBB, BLOCK), BF),
             pltpu.VMEM((ROWS, share, BLOCK), F32),
-            pltpu.VMEM((N, tokens, width), BF),
+            pltpu.VMEM((width, keys), F32),
             pltpu.VMEM((2, width, BLOCK), F32),
             pltpu.VMEM((tokens, BLOCK), F32),
             pltpu.VMEM((count, BLOCK), F32),
@@ -482,13 +560,45 @@
             pltpu.VMEM((2, ROWS, NBB, count), BF),
             pltpu.VMEM((2,) + bucket.shape, jnp.int32),
             pltpu.VMEM((2,) + bucket.shape, jnp.int32),
+            pltpu.VMEM((1, model), F32),
+            pltpu.VMEM(bucket.shape, jnp.int32),
+            pltpu.VMEM(bucket.shape, jnp.int32),
+            pltpu.VMEM(flat, F32),
+            pltpu.VMEM(flat, F32),
+            pltpu.VMEM(flat, F32),
+            pltpu.VMEM(flat, F32),
+            pltpu.VMEM((tokens, BLOCK), F32),
             dma((N,)), dma((N,)), dma((8,)), dma((8,)), dma((N,)), dma((N,)), dma((N,)), dma((N,)),
-            dma((2 * N,)), dma((2 * N,)), dma((N,)), dma((N,)), dma((8,)), dma((8,)), dma((8,)),
+            dma((2 * N,)), dma((2 * N,)), dma((N,)), dma((N,)), dma((8,)), dma((8,)), dma((8,)), dma((8,)),
         ],
         compiler_params=pltpu.CompilerParams(
             collective_id=0, has_side_effects=True, vmem_limit_bytes=60 * 1024 * 1024),
         name="step",
-    )(hidden_states, gain.reshape(1, model), key_weight, key_cotangent, bucket, sign_bits, momentum.reshape(flat), error.reshape(flat))
+    )(hidden_states, gain_row, key_weight, key_cotangent, bucket, sign_bits, momentum.reshape(flat), error.reshape(flat))
+    grad, momentum_new, error_new, update = pl.pallas_call(
+        results_kernel,
+        out_shape=(
+            jax.ShapeDtypeStruct((tokens, model), BF),
+            jax.ShapeDtypeStruct(flat, F32),
+            jax.ShapeDtypeStruct(flat, F32),
+            jax.ShapeDtypeStruct((width, keys), F32),
+        ),
+        in_specs=[any_spec] * 7,
+        out_specs=(any_spec,) * 4,
+        scratch_shapes=[
+            pltpu.VMEM((N, tokens, width), BF),
+            pltpu.VMEM((tokens, model), BF),
+            pltpu.VMEM((tokens, model), BF),
+            pltpu.VMEM((1, model), F32),
+            pltpu.VMEM((tokens, BLOCK), F32),
+            pltpu.VMEM(flat, F32),
+            pltpu.VMEM(flat, F32),
+            pltpu.VMEM((width, keys), F32),
+            dma((8,)), dma((8,)), dma((8,)), dma((5,)), dma((3,)),
+        ],
+        compiler_params=pltpu.CompilerParams(vmem_limit_bytes=60 * 1024 * 1024),
+        name="tail",
+    )(returned, hidden_states, gain_row, factor, momentum_new, error_new, update)
     return grad, momentum_new.reshape(momentum.shape), error_new.reshape(error.shape), update
 
 

time: 75.4 us -> 68.7 us (0.911)
  local copies, waits for them, and re-layouts: 5.4 us -> 0 us
  Pallas kernels: 69.1 us -> 68 us
    unnamed x10 -> x0, local copies, waits for them, and re-layouts: 5.4 us -> none
    pallas_call x1, Pallas kernels: 69.1 us -> 64.1 us  [on_device(): pl.pallas_call(functools.partial(kernel, scale), out_shape=(jax.ShapeDtyp...]
    pallas_call x0 -> x1, Pallas kernels: none -> 3.87 us  [on_device(): pl.pallas_call(results_kernel, out_shape=(jax.ShapeDtypeStruct((tokens, m...]
where the time goes in v3:
time: 68.7 us; the launch traced here: 68.6 us
  Pallas kernels  68 us (99%)
    pallas_call x1, Pallas kernels, on_device(): pl.pallas_call(functools.partial(kernel, scale), out_shape=(jax.ShapeDtyp...  64.1 us
    pallas_call x1, Pallas kernels, on_device(): pl.pallas_call(results_kernel, out_shape=(jax.ShapeDtypeStruct((tokens, m...  3.87 us

profile of v3, /device:TPU:1, one launch (start us, length us, event | category | flops | bytes accessed | tf_op | source)
XLA Modules:
  0.0 68.6 jit_solution(6121221603764522341)
XLA Ops:
  0.6 64.1 %step.1 = (bf16[16,128,512]{2,1,0:T(8,128)(2,1)}, f32[5,16,128]{2,1,0:T(8,128)}, f32[5,16,128]{2,1,0:T(8,128)}, f32[512,512]{1,0:T(8,128)}, f32[128,128]{1,0:T(8,128)}) custom-call(bf16[128,8192]{1,0:T(8,128)(2,1)} %hs_hbm.3, f32[1,8192]{1,0:T(1,128)} %bitcast.5, bf16[512,512]{1,0:T(8,128)(2,1)} %kw_hbm.1, bf16[128,512]{1,0:T(8,128)(2,1)} %cot_hbm.1, ...), custom_call_target="tpu_custom_call" | custom-call | tf_op jit(solution)/shard_map/step/pallas_call | solution.py:528
  64.7 3.9 %tail.1 = (bf16[128,8192]{1,0:T(8,128)(2,1)}, f32[5,16,128]{2,1,0:T(8,128)}, f32[5,16,128]{2,1,0:T(8,128)}, f32[512,512]{1,0:T(8,128)}) custom-call(bf16[16,128,512]{2,1,0:T(8,128)(2,1)} %get-tuple-element.13.ig_hbm, bf16[128,8192]{1,0:T(8,128)(2,1)} %hs_hbm.3, f32[1,8192]{1,0:T(1,128)} %bitcast.6, f32[128,128]{1,0:T(8,128)} %get-tuple-element.14.fac_hbm, ...), custom_call_target="tpu_custom_call" | custom-call | tf_op jit(solution)/shard_map/tail/pallas_call | solution.py:578

commit v4 on v3

--- a/solution.py
+++ b/solution.py
@@ -51,7 +51,7 @@
     ig_hbm, mom_out, err_out, upd_hbm, fac_out,
     hs_v, hs_rx, cot_v, cot_rx, kw_v, ig_tx, ig_rx, acc, blk, blk2, sel, table_bf, rs_rx, e_all,
     e_mid, upd_v, gcol, inv_v, ublk, ublk2, sel_h, bucket_h, bits_h,
-    gain_ref, bucket_ref, bits_ref, mom_ref, err_ref, mom_new, err_new, fac_v,
+    gain_ref, bucket_ref, bits_ref, mom_ref, err_ref, mom_new, err_new, fac_v, e_cols,
     load_sem, out_sem, cot_tx_s, cot_s, hs_tx_s, hs_s, ig_tx_s, ig_s, rs_tx_s, rs_s, ag_tx_s, ag_s, misc_s,
     shared_tx_s, shared_s, small_s,
 ):
@@ -120,12 +120,6 @@
     cot_load = pltpu.make_async_copy(cot_hbm, cot_v, misc_s.at[0])
     pairs = [(gain_hbm, gain_ref), (bucket_hbm, bucket_ref), (bits_hbm, bits_ref), (mom_hbm, mom_ref), (err_hbm, err_ref)]
     small_loads = [pltpu.make_async_copy(src, dst, small_s.at[k]) for k, (src, dst) in enumerate(pairs)]
-    for copy in hs_loads:
-        copy.start()
-    cot_load.start()
-    for copy in small_loads:
-        copy.start()
-
     barrier = pltpu.get_barrier_semaphore()
     ready = 0
     for dc, p in offsets:
@@ -144,6 +138,12 @@
         pl.semaphore_signal(barrier, inc=1, device_id=partner[j], device_id_type=MESH)
         ready += 1
 
+    for copy in hs_loads:
+        copy.start()
+    cot_load.start()
+    for copy in small_loads:
+        copy.start()
+
     squares = jnp.zeros((tokens, BLOCK), F32)
     for s in range(N):
         hs_loads[s].wait()
@@ -279,11 +279,13 @@
         lax.fori_loop(0, blk.shape[0] // 256, to_halves, 0)
 
     def half_sketch(j, dx):
-        rows = pl.ds(pl.multiple_of(((unit[j] + dx) % 2) * (NBB // 2), NBB // 2), NBB // 2)
+        first = ((unit[j] + dx) % 2) * (N // 2)
+        rows = pl.ds(pl.multiple_of(first * share, NBB // 2), NBB // 2)
 
         def sketch_row(i, carry):
             both = dot(sel_h[j, i, rows, :], blk2[...], PLAIN)
-            table_bf[j, i, rows, :] = (both[:, :BLOCK] + both[:, BLOCK:]).astype(BF)
+            table_bf[j, pl.ds(first, N // 2), i] = (
+                (both[:, :BLOCK] + both[:, BLOCK:]).astype(BF).reshape(N // 2, share, BLOCK))
             return carry
 
         lax.fori_loop(0, ROWS, sketch_row, 0)
@@ -291,7 +293,7 @@
     def share_copy(j, k, off):
         index, place = owner(j, *off)
         return pltpu.make_async_remote_copy(
-            src_ref=table_bf.at[j, :, pl.ds(pl.multiple_of(index * share, share), share), :],
+            src_ref=table_bf.at[j, index],
             dst_ref=rs_rx.at[j * N + my_index[j]], send_sem=rs_tx_s.at[j * N + k],
             recv_sem=rs_s.at[j * N + my_index[j]],
             device_id=place, device_id_type=MESH)
@@ -341,8 +343,7 @@
             @pl.when(own_slab)
             def _():
                 pltpu.make_async_copy(
-                    table_bf.at[0, :, pl.ds(pl.multiple_of(my_index[0] * share, share), share), :],
-                    rs_rx.at[my_index[0]], rs_s.at[my_index[0]]).start()
+                    table_bf.at[0, my_index[0]], rs_rx.at[my_index[0]], rs_s.at[my_index[0]]).start()
                 send_input_grad(0)
 
     for j in range(2):
@@ -364,11 +365,11 @@
     out_copies = [pltpu.make_async_copy(mom_new, mom_out, small_s.at[5])]
     out_copies[0].start()
     e_mid[...] = error_sum
-    e_all[:, mine, :] = error_sum.astype(BF)
+    e_all[dp] = error_sum.astype(BF)
     ag_sends = []
     for k, off in enumerate(DP_ORDER):
         ag_sends.append(pltpu.make_async_remote_copy(
-            src_ref=e_all.at[:, mine, :], dst_ref=e_all.at[:, mine, :], send_sem=ag_tx_s.at[k],
+            src_ref=e_all.at[dp], dst_ref=e_all.at[dp], send_sem=ag_tx_s.at[k],
             recv_sem=ag_s.at[dp], device_id=(dp_peer(*off), me), device_id_type=MESH))
     for copy in ag_sends:
         copy.start()
@@ -406,14 +407,16 @@
 
     for off in DP_ORDER:
         index = dp_peer(*off)
-        theirs = pl.ds(pl.multiple_of(index * share, share), share)
         pltpu.make_async_remote_copy(
-            src_ref=e_all.at[:, theirs, :], dst_ref=e_all.at[:, theirs, :], send_sem=misc_s.at[3],
+            src_ref=e_all.at[index], dst_ref=e_all.at[index], send_sem=misc_s.at[3],
             recv_sem=ag_s.at[index], device_id=(index, me), device_id_type=MESH).wait_recv()
+
+    for j in range(ROWS):
+        e_cols[j] = jnp.transpose(e_all[:, j].reshape(NBB, BLOCK))
 
     def estimate(i, carry):
         start = pl.multiple_of(i * 512, 512)
-        reads = [dot(e_all[j], sel[j, :, pl.ds(start, 512)], FIRST) for j in range(ROWS)]
+        reads = [dot(e_cols[j], sel[j, :, pl.ds(start, 512)], PLAIN) for j in range(ROWS)]
         middle = middle_five(reads)
         update = jnp.transpose(middle - jnp.clip(middle, -THRESHOLD, THRESHOLD))
         rows = pl.ds(start, 512)
@@ -423,7 +426,7 @@
         ublk2[rows, BLOCK:] = lower
         return carry
 
-    lax.fori_loop(0, ublk.shape[0] // 512, estimate, 0)
+    lax.fori_loop(0, ublk.shape[0] // 512, estimate, 0, unroll=True)
     for q in range(parts):
         upd_v[:, q * BLOCK:(q + 1) * BLOCK] = ublk[pl.ds(q, width, stride=parts), :]
     upd_store = pltpu.make_async_copy(upd_v, upd_hbm, misc_s.at[6])
@@ -548,9 +551,9 @@
             pltpu.VMEM((count, BLOCK), F32),
             pltpu.VMEM((count, 2 * BLOCK), BF),
             pltpu.VMEM((ROWS, NBB, count), BF),
-            pltpu.VMEM((2, ROWS, NBB, BLOCK), BF),
+            pltpu.VMEM((2, N, ROWS, share, BLOCK), BF),
             pltpu.VMEM((2 * N, ROWS, share, BLOCK), BF),
-            pltpu.VMEM((ROWS, NBB, BLOCK), BF),
+            pltpu.VMEM((N, ROWS, share, BLOCK), BF),
             pltpu.VMEM((ROWS, share, BLOCK), F32),
             pltpu.VMEM((width, keys), F32),
             pltpu.VMEM((2, width, BLOCK), F32),
@@ -568,6 +571,7 @@
             pltpu.VMEM(flat, F32),
             pltpu.VMEM(flat, F32),
             pltpu.VMEM((tokens, BLOCK), F32),
+            pltpu.VMEM((ROWS, BLOCK, NBB), BF),
             dma((N,)), dma((N,)), dma((8,)), dma((8,)), dma((N,)), dma((N,)), dma((N,)), dma((N,)),
             dma((2 * N,)), dma((2 * N,)), dma((N,)), dma((N,)), dma((8,)), dma((8,)), dma((8,)), dma((8,)),
         ],

time: 68.7 us -> 67.9 us (0.988)
  Pallas kernels: 68 us -> 67.1 us
    pallas_call x1, Pallas kernels: 64.1 us -> 63.3 us  [on_device(): pl.pallas_call(functools.partial(kernel, scale), out_shape=(jax.ShapeDtyp...]
where the time goes in v4:
time: 67.9 us; the launch traced here: 67.7 us
  Pallas kernels  67.1 us (99%)
    pallas_call x1, Pallas kernels, on_device(): pl.pallas_call(functools.partial(kernel, scale), out_shape=(jax.ShapeDtyp...  63.3 us
    pallas_call x1, Pallas kernels, on_device(): pl.pallas_call(results_kernel, out_shape=(jax.ShapeDtypeStruct((tokens, m...  3.83 us

profile of v4, /device:TPU:1, one launch (start us, length us, event | category | flops | bytes accessed | tf_op | source)
XLA Modules:
  0.0 67.7 jit_solution(10145889338952104498)
XLA Ops:
  0.6 63.3 %step.1 = (bf16[16,128,512]{2,1,0:T(8,128)(2,1)}, f32[5,16,128]{2,1,0:T(8,128)}, f32[5,16,128]{2,1,0:T(8,128)}, f32[512,512]{1,0:T(8,128)}, f32[128,128]{1,0:T(8,128)}) custom-call(bf16[128,8192]{1,0:T(8,128)(2,1)} %hs_hbm.3, f32[1,8192]{1,0:T(1,128)} %bitcast.5, bf16[512,512]{1,0:T(8,128)(2,1)} %kw_hbm.1, bf16[128,512]{1,0:T(8,128)(2,1)} %cot_hbm.1, ...), custom_call_target="tpu_custom_call" | custom-call | tf_op jit(solution)/shard_map/step/pallas_call | solution.py:531
  63.9 3.8 %tail.1 = (bf16[128,8192]{1,0:T(8,128)(2,1)}, f32[5,16,128]{2,1,0:T(8,128)}, f32[5,16,128]{2,1,0:T(8,128)}, f32[512,512]{1,0:T(8,128)}) custom-call(bf16[16,128,512]{2,1,0:T(8,128)(2,1)} %get-tuple-element.13.ig_hbm, bf16[128,8192]{1,0:T(8,128)(2,1)} %hs_hbm.3, f32[1,8192]{1,0:T(1,128)} %bitcast.6, f32[128,128]{1,0:T(8,128)} %get-tuple-element.14.fac_hbm, ...), custom_call_target="tpu_custom_call" | custom-call | tf_op jit(solution)/shard_map/tail/pallas_call | solution.py:582
